TPU v7x, 32 devices: a whole 2x2x4 slice. The times are simulated.
32 devices in a mesh: shard: 8 (over y, x, core), width: 4 (over z).
Axes of the slice: x: 2, y: 2, z: 4, core: 2. Of those that a mesh axis runs over, the one named last changes fastest.
Arguments:
- w_query: bfloat16 [5120, 5120], P('shard', 'width'), may hold values from -0.125 to 0.125
- low_query: bfloat16 [5120, 32], P('shard'), may hold values from -0.078125 to 0.078125
- high_query: bfloat16 [32, 5120], P(None, 'width'), may hold values from -1 to 1
- w_key: bfloat16 [5120, 5120], P('shard', 'width'), may hold values from -0.125 to 0.125
- low_key: bfloat16 [5120, 32], P('shard'), may hold values from -0.078125 to 0.078125
- high_key: bfloat16 [32, 5120], P(None, 'width'), may hold values from -1 to 1
- w_value: bfloat16 [5120, 5120], P('shard', 'width'), may hold values from -0.125 to 0.125
- low_value: bfloat16 [5120, 32], P('shard'), may hold values from -0.078125 to 0.078125
- high_value: bfloat16 [32, 5120], P(None, 'width'), may hold values from -1 to 1
- norm_train: float32 [5120], P(('shard', 'width')), may hold values from 0.25 to 1.75
- norm_step: float32 [5120], P(('shard', 'width')), may hold values from -0.3 to 0.3
Outputs:
- ready_query: bfloat16 [5120, 5120], P(None, 'width')
- ready_key: bfloat16 [5120, 5120], P(None, 'width')
- ready_value: bfloat16 [5120, 5120], P(None, 'width')
- factor_query: float32 [5120], P('width')
- factor_key: float32 [5120], P('width')
- factor_value: float32 [5120], P('width')
- serve_norm: bfloat16 [5120], replicated
All inputs are finite; a program needn't handle non-finite values. Where the computation divides by a largest or mean magnitude, that divisor is 1e-20 or more.
Results may differ from a plain program's by a relative error of at most 0.001.
Values may be sent and summed in bfloat16 or wider, within the bound.
A program may use at most 128 MiB of HBM per device.

v0:
```python
import functools

import jax
import jax.numpy as jnp
from jax import lax
from jax.experimental import pallas as pl
from jax.experimental.pallas import tpu as pltpu
from jax.sharding import PartitionSpec as P

mix_rate = 0.5
MESH = pl.DeviceIdType.MESH
ANY = pl.BlockSpec(memory_space=pl.ANY)


def chunks_of(rows):
    for count in (5, 4, 2):
        if rows % (2 * count * 16) == 0:
            return count
    return 1


def gather_kernel(n, width, *refs):
    weights, lows, highs, norms = refs[0:3], refs[3:6], refs[6:9], refs[9:11]
    ready, small_outs = refs[11], refs[12:16]
    w_mem, low_mem, high_mem, norm_mem, latest, scale, maxima = refs[16:23]
    load_sem, send_sem, max_send, max_recv, norm_send, norm_recv = refs[23:29]
    ring_sem, pair_sem, low_turned, held, gains, out_sem = refs[29:35]
    outs = [ready.at[m] for m in range(3)]

    rows = w_mem.shape[1]
    chips = n // 2
    half = chips // 2
    count = chunks_of(rows)
    piece = rows // (2 * count)
    steps = 3 * count

    me = lax.axis_index("shard")
    line = lax.axis_index("width")
    chip, core = me // 2, lax.rem(me, 2)
    sibling = me + 1 - 2 * core

    def turned(c):
        return jnp.where(c < half, c, chips + half - 1 - c)

    place = turned(chip)

    def shard_at(offset):
        return turned(lax.rem(place + offset + 2 * chips, chips)) * 2 + core

    loads = []
    for m in range(3):
        group = []
        for source, target in (
            (weights[m], w_mem.at[m]),
            (lows[m], low_turned.at[m]),
            (highs[m], high_mem.at[m]),
        ):
            group.append(pltpu.make_async_copy(source, target, load_sem.at[m, len(group)]))
        loads.append(group)
    norm_loads = [
        pltpu.make_async_copy(norms[i], norm_mem.at[i], load_sem.at[3, i]) for i in range(2)
    ]
    for group in loads:
        for copy in group:
            copy.start()
    for copy in norm_loads:
        copy.start()

    barrier = pltpu.get_barrier_semaphore()
    for step in range(1, n):
        pl.semaphore_signal(
            barrier, inc=1, device_id={"shard": lax.rem(me + step, n)}, device_id_type=MESH
        )
    for step in range(1, width):
        pl.semaphore_signal(
            barrier, inc=1, device_id={"width": lax.rem(line + step, width)}, device_id_type=MESH
        )

    tile = piece

    def merge(m):
        for copy in loads[m]:
            copy.wait()
        low_mem[m] = low_turned[m].T

        def body(t, largest):
            at = pl.ds(pl.multiple_of(t * tile, tile), tile)
            value = w_mem[m, at, :].astype(jnp.float32) + mix_rate * jnp.dot(
                low_mem[m, at, :], high_mem[m], preferred_element_type=jnp.float32
            )
            latest[m, at, :] = value
            sizes = jnp.abs(value).reshape(tile // 8, 8, value.shape[1])
            return jnp.maximum(largest, jnp.max(sizes, axis=0))

        largest = lax.fori_loop(0, rows // tile, body, jnp.zeros((8, w_mem.shape[2]), jnp.float32))
        maxima[m, me] = jnp.max(largest, axis=0, keepdims=True)

    def share(m):
        for step in range(1, n):
            pltpu.make_async_remote_copy(
                src_ref=maxima.at[m, me],
                dst_ref=maxima.at[m, me],
                send_sem=max_send.at[m],
                recv_sem=max_recv.at[m],
                device_id={"shard": lax.rem(me + step, n)},
                device_id_type=MESH,
            ).start()

    def settle(m):
        others = maxima.at[m, pl.ds(0, n - 1)]
        pltpu.make_async_copy(others, others, max_recv.at[m]).wait()
        factor = jnp.max(maxima[m], axis=0)
        held[m] = factor
        scale[m] = 1.0 / factor

    def rows_of(letter, k):
        return ((letter * count) + k % count) * piece

    def finish(k):
        m = k // count
        for letter in range(2):
            at = pl.ds(rows_of(letter, k), piece)
            ready[m, me, at, :] = (latest[m, at, :] * scale[m]).astype(jnp.bfloat16)

    def view(k, letter, owner):
        return outs[k // count].at[owner, pl.ds(rows_of(letter, k), piece)]

    def ring_copy(k, side, letter, hop):
        sign = 1 - 2 * side
        owner = shard_at(-sign * hop)
        where = view(k, letter, owner)
        return pltpu.make_async_remote_copy(
            src_ref=where,
            dst_ref=where,
            send_sem=send_sem.at[k // count],
            recv_sem=ring_sem.at[k, side, letter, hop],
            device_id={"shard": shard_at(sign)},
            device_id_type=MESH,
        )

    def ring_arrival(k, side, letter, hop):
        sign = 1 - 2 * side
        owner = shard_at(-sign * (hop + 1))
        where = view(k, letter, owner)
        pltpu.make_async_copy(where, where, ring_sem.at[k, side, letter, hop]).wait()
        return owner

    def pair_copy(k, letter, owner):
        where = view(k, letter, owner)
        pltpu.make_async_remote_copy(
            src_ref=where,
            dst_ref=where,
            send_sem=send_sem.at[k // count],
            recv_sem=pair_sem.at[k // count],
            device_id={"shard": sibling},
            device_id_type=MESH,
        ).start()

    def hops(side, letter):
        return half if side == letter else half - 1

    small_writes = [
        pltpu.make_async_copy(held.at[m], small_outs[m], out_sem.at[m]) for m in range(3)
    ] + [pltpu.make_async_copy(gains, small_outs[3], out_sem.at[3])]
    merge(0)
    pl.semaphore_wait(barrier, n - 1 + width - 1)
    share(0)
    settle(0)
    finish(0)

    for j in range(steps + half + 1):
        if j < steps:
            for side in range(2):
                if hops(side, side) > 0:
                    ring_copy(j, side, side, 0).start()
        for hop in range(half):
            k = j - 1 - hop
            if 0 <= k < steps and hop + 1 < half:
                for side in range(2):
                    owner = ring_arrival(k, side, side, hop)
                    ring_copy(k, side, side, hop + 1).start()
                    pair_copy(k, side, owner)
        if j < steps:
            for side in range(2):
                if hops(side, 1 - side) > 0:
                    ring_copy(j, side, 1 - side, 0).start()
        for hop in range(half - 1):
            k = j - 1 - hop
            if 0 <= k < steps and hop + 1 < half - 1:
                for side in range(2):
                    owner = ring_arrival(k, side, 1 - side, hop)
                    ring_copy(k, side, 1 - side, hop + 1).start()
                    pair_copy(k, 1 - side, owner)
        if j < steps:
            for letter in range(2):
                pair_copy(j, letter, me)
        if j == 0:
            merge(1)
            share(1)
            for copy in norm_loads:
                copy.wait()
            gains[me, line] = norm_mem[0] + norm_mem[1]
            for step in range(1, width):
                pltpu.make_async_remote_copy(
                    src_ref=gains.at[me, line],
                    dst_ref=gains.at[me, line],
                    send_sem=norm_send.at[0],
                    recv_sem=norm_recv.at[0],
                    device_id={"width": lax.rem(line + step, width)},
                    device_id_type=MESH,
                ).start()
        if j == 1:
            merge(2)
            share(2)
            ours = gains.at[me, pl.ds(0, width - 1)]
            if width > 1:
                pltpu.make_async_copy(ours, ours, norm_recv.at[0]).wait()
            for step in range(1, n):
                pltpu.make_async_remote_copy(
                    src_ref=gains.at[me],
                    dst_ref=gains.at[me],
                    send_sem=norm_send.at[1],
                    recv_sem=norm_recv.at[1],
                    device_id={"shard": lax.rem(me + step, n)},
                    device_id_type=MESH,
                ).start()
        if j == steps - 1:
            block = gains.at[pl.ds(0, n - 1)]
            pltpu.make_async_copy(block, block, norm_recv.at[1]).wait()
            for copy in small_writes:
                copy.start()
        if j + 1 < steps:
            if (j + 1) % count == 0:
                settle((j + 1) // count)
            finish(j + 1)
        for side in range(2):
            for letter in (side, 1 - side):
                hop = hops(side, letter) - 1
                k = j - 2 - hop
                if hop >= 0 and 0 <= k < steps:
                    owner = ring_arrival(k, side, letter, hop)
                    pair_copy(k, letter, owner)

    for m in range(3):
        theirs = outs[m].at[pl.ds(0, chips)]
        pltpu.make_async_copy(theirs, theirs, pair_sem.at[m]).wait()
        sent = outs[m].at[pl.ds(0, n - 1)]
        pltpu.make_async_copy(sent, sent, send_sem.at[m]).wait()
        others = maxima.at[m, pl.ds(0, n - 1)]
        pltpu.make_async_copy(others, others, max_send.at[m]).wait()
    ours = gains.at[me, pl.ds(0, width - 1)]
    pltpu.make_async_copy(ours, ours, norm_send.at[0]).wait()
    block = gains.at[pl.ds(0, n - 1)]
    pltpu.make_async_copy(block, block, norm_send.at[1]).wait()
    for copy in small_writes:
        copy.wait()


def place_kernel(*refs):
    source, small = refs[0], refs[1:5]
    targets, finals, sem = refs[5:8], refs[8:12], refs[12]
    factors, gains, small_sem = refs[13:16], refs[16], refs[17]
    scales, serve = refs[18:21], refs[21]
    writes = [
        pltpu.make_async_copy(refs[18 + i], finals[i], small_sem.at[4 + i]) for i in range(4)
    ]
    loads = [
        pltpu.make_async_copy(small[i], refs[13 + i], small_sem.at[i]) for i in range(4)
    ]
    for copy in loads:
        copy.start()
    copies = []
    for m in range(3):
        for i in range(source.shape[1]):
            copies.append(
                pltpu.make_async_copy(source.at[m, i], targets[m].at[i], sem.at[m, i])
            )
    for copy in copies:
        copy.start()
    for copy in loads:
        copy.wait()
    for m in range(3):
        scales[m][...] = factors[m][...].reshape(scales[m].shape)
    blocks = [gains[i, k] for i in range(gains.shape[0]) for k in range(gains.shape[1])]
    line = jnp.concatenate(blocks, axis=1)
    serve[...] = line.reshape(serve.shape).astype(jnp.bfloat16)
    copies[0].wait()
    for copy in writes:
        copy.start()
    for copy in copies[1:] + writes:
        copy.wait()


def body(n, width, w_query, low_query, high_query, w_key, low_key, high_key, w_value, low_value, high_value, norm_train, norm_step):
    rows, columns = w_query.shape
    rank = low_query.shape[1]
    length = norm_train.shape[0]
    half = n // 4
    steps = 3 * chunks_of(rows)
    results = pl.pallas_call(
        functools.partial(gather_kernel, n, width),
        name="merge_gather",
        out_shape=[pltpu.VMEM((3, n, rows, columns), jnp.bfloat16)]
        + [jax.ShapeDtypeStruct((1, columns), jnp.float32)] * 3
        + [jax.ShapeDtypeStruct((n, width, 1, length), jnp.float32)],
        in_specs=[ANY] * 11,
        out_specs=[pl.BlockSpec(memory_space=pltpu.VMEM)]
        + [pl.BlockSpec(memory_space=pltpu.HBM)] * 4,
        scratch_shapes=[
            pltpu.VMEM((3, rows, columns), jnp.bfloat16),
            pltpu.VMEM((3, rows, rank), jnp.bfloat16),
            pltpu.VMEM((3, rank, columns), jnp.bfloat16),
            pltpu.VMEM((2, 1, length), jnp.float32),
            pltpu.VMEM((3, rows, columns), jnp.float32),
            pltpu.VMEM((3, 1, columns), jnp.float32),
            pltpu.VMEM((3, n, 1, columns), jnp.float32),
            pltpu.SemaphoreType.DMA((4, 3)),
            pltpu.SemaphoreType.DMA((3,)),
            pltpu.SemaphoreType.DMA((3,)),
            pltpu.SemaphoreType.DMA((3,)),
            pltpu.SemaphoreType.DMA((2,)),
            pltpu.SemaphoreType.DMA((2,)),
            pltpu.SemaphoreType.DMA((steps, 2, 2, half)),
            pltpu.SemaphoreType.DMA((3,)),
            pltpu.VMEM((3, rank, rows), jnp.bfloat16),
            pltpu.VMEM((3, 1, columns), jnp.float32),
            pltpu.VMEM((n, width, 1, length), jnp.float32),
            pltpu.SemaphoreType.DMA((4,)),
        ],
        compiler_params=pltpu.CompilerParams(
            collective_id=0, has_side_effects=True, vmem_limit_bytes=20 * 2**20
        ),
    )(
        w_query, w_key, w_value,
        low_query.T, low_key.T, low_value.T,
        high_query, high_key, high_value,
        norm_train.reshape(1, length), norm_step.reshape(1, length),
    )
    placed = pl.pallas_call(
        place_kernel,
        name="place",
        out_shape=[jax.ShapeDtypeStruct((n, rows, columns), jnp.bfloat16)] * 3
        + [jax.ShapeDtypeStruct((columns,), jnp.float32)] * 3
        + [jax.ShapeDtypeStruct((n * width * length,), jnp.bfloat16)],
        in_specs=[ANY] + [pl.BlockSpec(memory_space=pltpu.HBM)] * 4,
        out_specs=[ANY] * 3 + [pl.BlockSpec(memory_space=pltpu.HBM)] * 4,
        scratch_shapes=[
            pltpu.SemaphoreType.DMA((3, n)),
            *[pltpu.VMEM((1, columns), jnp.float32)] * 3,
            pltpu.VMEM((n, width, 1, length), jnp.float32),
            pltpu.SemaphoreType.DMA((8,)),
            *[pltpu.VMEM((columns,), jnp.float32)] * 3,
            pltpu.VMEM((n * width * length,), jnp.bfloat16),
        ],
        compiler_params=pltpu.CompilerParams(vmem_limit_bytes=2**20),
    )(pltpu.with_memory_space_constraint(results[0], pltpu.VMEM), *(pltpu.with_memory_space_constraint(small, pltpu.HBM) for small in results[1:]))
    return (
        *(ready.reshape(n * rows, columns) for ready in placed[0:3]),
        *placed[3:],
    )


def solution(mesh):
    n, width = mesh.shape["shard"], mesh.shape["width"]
    return jax.shard_map(
        functools.partial(body, n, width),
        mesh=mesh,
        in_specs=(
            P("shard", "width"),
            P("shard", None),
            P(None, "width"),
            P("shard", "width"),
            P("shard", None),
            P(None, "width"),
            P("shard", "width"),
            P("shard", None),
            P(None, "width"),
            P(("shard", "width")),
            P(("shard", "width")),
        ),
        out_specs=(
            P(None, "width"),
            P(None, "width"),
            P(None, "width"),
            P("width"),
            P("width"),
            P("width"),
            P(),
        ),
        check_vma=False,
    )
```

profile of v0, /device:TPU:0, one launch (start us, length us, event | category | flops | bytes accessed | tf_op | source)
XLA Modules:
  0.0 186.4 jit_solution(6383398306800230098)
XLA Ops:
  0.6 172.8 %merge_gather.1 = (bf16[3,8,640,1280]{3,2,1,0:T(8,128)(2,1)S(1)}, f32[1,1280]{1,0:T(1,128)}, f32[1,1280]{1,0:T(1,128)}, f32[1,1280]{1,0:T(1,128)}, f32[8,4,1,160]{3,2,1,0:T(1,128)}) custom-call(bf16[640,1280]{1,0:T(8,128)(2,1)} %refs_0_.1, bf16[640,1280]{1,0:T(8,128)(2,1)} %refs_1_.1, bf16[640,1280]{1,0:T(8,128)(2,1)} %refs_2_.1, bf16[32,640]{1,0:T(8,128)(2,1)} %bitcast.8, ...), custom_call_target="tpu_custom_call" | custom-call | tf_op jit(solution)/shard_map/merge_gather/pallas_call | solution.py:300
  173.4 12.9 %place.1 = (bf16[8,640,1280]{2,1,0:T(8,128)(2,1)}, bf16[8,640,1280]{2,1,0:T(8,128)(2,1)}, bf16[8,640,1280]{2,1,0:T(8,128)(2,1)}, f32[1280]{0:T(1024)}, f32[1280]...) custom-call(bf16[3,8,640,1280]{3,2,1,0:T(8,128)(2,1)S(1)} %get-tuple-element.19.refs_0_, ...), custom_call_target="tpu_custom_call" | custom-call | tf_op jit(solution)/shard_map/place/pallas_call | solution.py:339
where the time goes:
time: 187 us; the launch traced here: 186 us
  Pallas kernels  186 us (99%)
    pallas_call x1, Pallas kernels, body(): pl.pallas_call(functools.partial(gather_kernel, n, width), name='merge_ga...  173 us
    pallas_call x1, Pallas kernels, body(): pl.pallas_call(place_kernel, name='place', out_shape=[jax.ShapeDtypeStruc...  12.9 us

commit v1 on v0

v1 whole, which is shorter than its diff:
```python
import functools

import jax
import jax.numpy as jnp
from jax import lax
from jax.experimental import pallas as pl
from jax.experimental.pallas import tpu as pltpu
from jax.sharding import PartitionSpec as P

mix_rate = 0.5
MESH = pl.DeviceIdType.MESH
ANY = pl.BlockSpec(memory_space=pl.ANY)


def chunks_of(rows):
    for count in (5, 4, 2):
        if rows % (2 * count * 16) == 0:
            return count
    return 1


def raw_steps(rows):
    return min(2, chunks_of(rows))


def gather_kernel(n, width, *refs):
    weights, lows, highs, norms = refs[0:3], refs[3:6], refs[6:9], refs[9:11]
    ready, small_outs = refs[11], refs[12:16]
    w_mem, low_mem, high_mem, norm_mem, latest, scale, largest_of = refs[16:23]
    load_sem, ring_send, pair_send, max_send, max_recv, norm_send, norm_recv = refs[23:30]
    ring_sem, pair_sem, low_turned, held, gains, out_sem = refs[30:36]
    low_raw, low_far, raw_send, low_send, low_recv, max_in, line_send, line_recv = refs[36:44]
    outs = [ready.at[m] for m in range(3)]

    rows = w_mem.shape[1]
    chips = n // 2
    half = chips // 2
    count = chunks_of(rows)
    piece = rows // (2 * count)
    steps = 3 * count
    raw = raw_steps(rows)
    raw_rows = 2 * piece * raw
    reach = low_raw.shape[2]
    rounds = n.bit_length() - 1
    assert n == 1 << rounds

    me = lax.axis_index("shard")
    line = lax.axis_index("width")
    chip, core = me // 2, lax.rem(me, 2)
    sibling = me + 1 - 2 * core

    def turned(c):
        return jnp.where(c < half, c, chips + half - 1 - c)

    place = turned(chip)

    def shard_at(offset):
        return turned(lax.rem(place + offset + 2 * chips, chips)) * 2 + core

    def group(r):
        return lax.div(me, 1 << r)

    def partner(r):
        return me + (1 << r) * (1 - 2 * lax.rem(group(r), 2))

    def load(source, target, m, slot):
        return pltpu.make_async_copy(source, target, load_sem.at[m, slot])

    first = load(weights[0].at[pl.ds(0, raw_rows)], w_mem.at[0, pl.ds(0, raw_rows)], 3, 2)
    loads = []
    for m in range(3):
        parts = [load(lows[m], low_turned.at[m], m, 0), load(highs[m], high_mem.at[m], m, 1)]
        if m > 0:
            parts.append(load(weights[m], w_mem.at[m], m, 2))
        elif raw_rows < rows:
            rest = pl.ds(raw_rows, rows - raw_rows)
            parts.append(load(weights[0].at[rest], w_mem.at[0, rest], m, 2))
        loads.append(parts)
    norm_loads = [load(norms[i], norm_mem.at[i], 3, i) for i in range(2)]
    first.start()

    barrier = pltpu.get_barrier_semaphore()

    def greet(axis, index):
        pl.semaphore_signal(barrier, inc=1, device_id={axis: index}, device_id_type=MESH)

    greet("shard", shard_at(1))
    greet("shard", shard_at(-1))
    for r in range(rounds):
        greet("shard", partner(r))

    @pl.when(line > 0)
    def _():
        greet("width", line - 1)

    @pl.when(line < width - 1)
    def _():
        greet("width", line + 1)

    for parts in loads:
        for copy in parts:
            copy.start()
    for copy in norm_loads:
        copy.start()

    tile = piece

    def merge(m):
        for copy in loads[m]:
            copy.wait()
        low_mem[m] = low_turned[m].T

        def body(t, largest):
            at = pl.ds(pl.multiple_of(t * tile, tile), tile)
            value = w_mem[m, at, :].astype(jnp.float32) + mix_rate * jnp.dot(
                low_mem[m, at, :], high_mem[m], preferred_element_type=jnp.float32
            )
            latest[m, at, :] = value
            sizes = jnp.abs(value).reshape(tile // 8, 8, value.shape[1])
            return jnp.maximum(largest, jnp.max(sizes, axis=0))

        largest = lax.fori_loop(0, rows // tile, body, jnp.zeros((8, w_mem.shape[2]), jnp.float32))
        largest_of[m, 0] = jnp.max(largest, axis=0, keepdims=True)
        max_copy(m, 0).start()

    def max_copy(m, r):
        return pltpu.make_async_remote_copy(
            src_ref=largest_of.at[m, r],
            dst_ref=max_in.at[m, r],
            send_sem=max_send.at[m, r],
            recv_sem=max_recv.at[m, r],
            device_id={"shard": partner(r)},
            device_id_type=MESH,
        )

    met = [0, 0, 0]

    def advance(m):
        r = met[m]
        if r == rounds:
            return
        max_copy(m, r).wait_recv()
        largest_of[m, r + 1] = jnp.maximum(largest_of[m, r], max_in[m, r])
        met[m] = r + 1
        if r + 1 < rounds:
            max_copy(m, r + 1).start()

    def settle(m):
        while met[m] < rounds:
            advance(m)
        factor = largest_of[m, rounds]
        held[m] = factor
        scale[m] = 1.0 / factor

    def gain_copy(r):
        return pltpu.make_async_remote_copy(
            src_ref=gains.at[line, pl.ds(group(r) * (1 << r), 1 << r)],
            dst_ref=gains.at[line, pl.ds(group(r) * (1 << r), 1 << r)],
            send_sem=norm_send.at[r],
            recv_sem=norm_recv.at[r],
            device_id={"shard": partner(r)},
            device_id_type=MESH,
        )

    def gain_arrival(r):
        theirs = gains.at[line, pl.ds(lax.div(partner(r), 1 << r) * (1 << r), 1 << r)]
        pltpu.make_async_copy(theirs, theirs, norm_recv.at[r]).wait()

    def line_copy(way, s):
        sign = 1 - 2 * way
        block = gains.at[line - sign * s]
        return pltpu.make_async_remote_copy(
            src_ref=block,
            dst_ref=block,
            send_sem=line_send.at[way, s],
            recv_sem=line_recv.at[way, s],
            device_id={"width": line + sign},
            device_id_type=MESH,
        )

    def inside(value):
        return (value >= 0) & (value < width)

    def line_start(way, s):
        sign = 1 - 2 * way

        @pl.when(inside(line - sign * s) & inside(line + sign))
        def _():
            line_copy(way, s).start()

    def line_finish(way, s):
        sign = 1 - 2 * way

        @pl.when(inside(line - sign * (s + 1)))
        def _():
            block = gains.at[line - sign * (s + 1)]
            pltpu.make_async_copy(block, block, line_recv.at[way, s]).wait()

        @pl.when(inside(line - sign * s) & inside(line + sign))
        def _():
            line_copy(way, s).wait_send()

    def gain_first():
        for copy in norm_loads:
            copy.wait()
        gains[line, me] = norm_mem[0] + norm_mem[1]
        gain_copy(0).start()

    def gain_round(r):
        gain_arrival(r)
        if r + 1 < rounds:
            gain_copy(r + 1).start()
        elif width > 1:
            for way in range(2):
                line_start(way, 0)

    def gain_line(s):
        for way in range(2):
            line_finish(way, s)
        if s + 1 < width - 1:
            for way in range(2):
                line_start(way, s + 1)

    errands = [gain_first]
    errands += [functools.partial(gain_round, r) for r in range(rounds)]
    errands += [functools.partial(gain_line, s) for s in range(width - 1)]

    def rows_of(letter, k):
        return (2 * (k % count) + letter) * piece

    def finish(k):
        m = k // count
        at = pl.ds(rows_of(0, k), 2 * piece)
        ready[m, me, at, :] = (latest[m, at, :] * scale[m]).astype(jnp.bfloat16)

    def view(k, letter, owner):
        return outs[k // count].at[owner, pl.ds(rows_of(letter, k), piece)]

    def ring_copy(k, side, letter, hop):
        sign = 1 - 2 * side
        owner = shard_at(-sign * hop)
        where = view(k, letter, owner)
        source = where
        if k < raw and hop == 0:
            source = w_mem.at[0, pl.ds(rows_of(letter, k), piece)]
        return pltpu.make_async_remote_copy(
            src_ref=source,
            dst_ref=where,
            send_sem=raw_send.at[k, side, letter, hop] if k < raw else ring_send.at[k // count],
            recv_sem=ring_sem.at[k, side, letter, hop],
            device_id={"shard": shard_at(sign)},
            device_id_type=MESH,
        )

    def low_copy(side, hop):
        sign = 1 - 2 * side
        where = low_raw.at[shard_at(-sign * hop)]
        return pltpu.make_async_remote_copy(
            src_ref=low_turned.at[0, :, pl.ds(0, reach)] if hop == 0 else where,
            dst_ref=where,
            send_sem=low_send.at[side, hop],
            recv_sem=low_recv.at[side, hop],
            device_id={"shard": shard_at(sign)},
            device_id_type=MESH,
        )

    def ring_start(k, side, letter, hop):
        ring_copy(k, side, letter, hop).start()

    def low_arrival(side, hop):
        sign = 1 - 2 * side
        owner = shard_at(-sign * (hop + 1))
        where = low_raw.at[owner]
        pltpu.make_async_copy(where, where, low_recv.at[side, hop]).wait()
        if hop + 1 < hops(side, 0):
            low_copy(side, hop + 1).start()
        low_far[owner] = low_raw[owner].T

    def ring_arrival(k, side, letter, hop):
        sign = 1 - 2 * side
        owner = shard_at(-sign * (hop + 1))
        where = view(k, letter, owner)
        pltpu.make_async_copy(where, where, ring_sem.at[k, side, letter, hop]).wait()
        return owner

    def pair_copy(k, letter, owner):
        where = view(k, letter, owner)
        pltpu.make_async_remote_copy(
            src_ref=where,
            dst_ref=where,
            send_sem=pair_send.at[k // count],
            recv_sem=pair_sem.at[k // count],
            device_id={"shard": sibling},
            device_id_type=MESH,
        ).start()

    def hops(side, letter):
        return half if side == letter else half - 1

    pending = []

    def landed(k, side, letter, hop, owner):
        if k < raw:
            pending.append((k, side, letter, hop, owner))
        else:
            pair_copy(k, letter, owner)

    low_seen = set()

    def absorb():
        for k, side, letter, hop, owner in pending:
            if hop + 1 < hops(side, letter):
                ring_copy(k, side, letter, hop + 1).wait_send()
            from_side, from_hop = (side, hop) if hop < hops(side, 0) else (0, half - 1)
            for h in range(from_hop + 1):
                if (from_side, h) not in low_seen:
                    low_seen.add((from_side, h))
                    low_arrival(from_side, h)
            at = pl.ds(rows_of(letter, k), piece)
            value = ready[0, owner, at, :].astype(jnp.float32) + mix_rate * jnp.dot(
                low_far[owner, at, :], high_mem[0], preferred_element_type=jnp.float32
            )
            ready[0, owner, at, :] = (value * scale[0]).astype(jnp.bfloat16)
            pair_copy(k, letter, owner)
        pending.clear()

    small_writes = [
        pltpu.make_async_copy(held.at[m], small_outs[m], out_sem.at[m]) for m in range(3)
    ] + [pltpu.make_async_copy(gains, small_outs[3], out_sem.at[3])]
    first.wait()
    pl.semaphore_wait(
        barrier,
        2 + rounds + (line > 0).astype(jnp.int32) + (line < width - 1).astype(jnp.int32),
    )

    for j in range(steps + half + 1):
        if j < steps:
            for side in range(2):
                if hops(side, side) > 0:
                    ring_start(j, side, side, 0)
        if j == 1:
            merge(1)
            advance(0)
        for hop in range(half):
            k = j - 1 - hop
            if 0 <= k < steps and hop + 1 < half:
                for side in range(2):
                    owner = ring_arrival(k, side, side, hop)
                    ring_start(k, side, side, hop + 1)
                    landed(k, side, side, hop, owner)
        if j < steps:
            for side in range(2):
                if hops(side, 1 - side) > 0:
                    ring_start(j, side, 1 - side, 0)
        for hop in range(half - 1):
            k = j - 1 - hop
            if 0 <= k < steps and hop + 1 < half - 1:
                for side in range(2):
                    owner = ring_arrival(k, side, 1 - side, hop)
                    ring_start(k, side, 1 - side, hop + 1)
                    landed(k, side, 1 - side, hop, owner)
        if raw <= j < steps:
            for letter in range(2):
                pair_copy(j, letter, me)
        if j == 0:
            merge(0)
            for side in range(2):
                if hops(side, 0) > 0:
                    low_copy(side, 0).start()
            advance(0)
        if j == raw:
            merge(2)
        for m in range(1, 3):
            if j > m and met[m] < rounds:
                advance(m)
        if 1 <= j < half:
            for side in range(2):
                if j - 1 < hops(side, 0):
                    low_seen.add((side, j - 1))
                    low_arrival(side, j - 1)
        if j > 0 and errands:
            errands.pop(0)()
        if j == steps - 1:
            while errands:
                errands.pop(0)()
            for copy in small_writes:
                copy.start()
        if raw <= j + 1 < steps:
            if j + 1 == raw:
                settle(0)
            if (j + 1) % count == 0:
                settle((j + 1) // count)
            finish(j + 1)
        for side in range(2):
            for letter in (side, 1 - side):
                hop = hops(side, letter) - 1
                k = j - 2 - hop
                if hop >= 0 and 0 <= k < steps:
                    owner = ring_arrival(k, side, letter, hop)
                    landed(k, side, letter, hop, owner)
        if j == raw:
            for k in range(raw):
                finish(k)
                for letter in range(2):
                    pair_copy(k, letter, me)
        if j >= raw:
            absorb()

    for m in range(3):
        theirs = outs[m].at[pl.ds(0, chips)]
        pltpu.make_async_copy(theirs, theirs, pair_sem.at[m]).wait()
        pltpu.make_async_copy(theirs, theirs, pair_send.at[m]).wait()
        kept = raw_rows if m == 0 else 0
        if kept < rows:
            sent = outs[m].at[pl.ds(0, chips - 1), pl.ds(kept, rows - kept)]
            pltpu.make_async_copy(sent, sent, ring_send.at[m]).wait()
        for r in range(rounds):
            max_copy(m, r).wait_send()
    for side in range(2):
        for k in range(raw):
            for letter in range(2):
                if hops(side, letter) > 0:
                    ring_copy(k, side, letter, 0).wait_send()
        for hop in range(hops(side, 0)):
            low_copy(side, hop).wait_send()
    for r in range(rounds):
        gain_copy(r).wait_send()
    for copy in small_writes:
        copy.wait()


def place_kernel(*refs):
    source, small = refs[0], refs[1:5]
    targets, finals, sem = refs[5:8], refs[8:12], refs[12]
    factors, gains, small_sem = refs[13:16], refs[16], refs[17]
    scales, serve = refs[18:21], refs[21]
    writes = [
        pltpu.make_async_copy(refs[18 + i], finals[i], small_sem.at[4 + i]) for i in range(4)
    ]
    loads = [
        pltpu.make_async_copy(small[i], refs[13 + i], small_sem.at[i]) for i in range(4)
    ]
    for copy in loads:
        copy.start()
    copies = []
    for m in range(3):
        for i in range(source.shape[1]):
            copies.append(
                pltpu.make_async_copy(source.at[m, i], targets[m].at[i], sem.at[m, i])
            )
    for copy in copies:
        copy.start()
    for copy in loads:
        copy.wait()
    for m in range(3):
        scales[m][...] = factors[m][...].reshape(scales[m].shape)
    blocks = [gains[k, i] for i in range(gains.shape[1]) for k in range(gains.shape[0])]
    line = jnp.concatenate(blocks, axis=1)
    serve[...] = line.reshape(serve.shape).astype(jnp.bfloat16)
    copies[0].wait()
    for copy in writes:
        copy.start()
    for copy in copies[1:] + writes:
        copy.wait()


def body(n, width, w_query, low_query, high_query, w_key, low_key, high_key, w_value, low_value, high_value, norm_train, norm_step):
    rows, columns = w_query.shape
    rank = low_query.shape[1]
    length = norm_train.shape[0]
    half = n // 4
    steps = 3 * chunks_of(rows)
    raw = raw_steps(rows)
    rounds = n.bit_length() - 1
    reach = min(rows, -(-(rows // chunks_of(rows)) * raw // 128) * 128)
    results = pl.pallas_call(
        functools.partial(gather_kernel, n, width),
        name="merge_gather",
        out_shape=[pltpu.VMEM((3, n, rows, columns), jnp.bfloat16)]
        + [jax.ShapeDtypeStruct((1, columns), jnp.float32)] * 3
        + [jax.ShapeDtypeStruct((width, n, 1, length), jnp.float32)],
        in_specs=[ANY] * 11,
        out_specs=[pl.BlockSpec(memory_space=pltpu.VMEM)]
        + [pl.BlockSpec(memory_space=pltpu.HBM)] * 4,
        scratch_shapes=[
            pltpu.VMEM((3, rows, columns), jnp.bfloat16),
            pltpu.VMEM((3, rows, rank), jnp.bfloat16),
            pltpu.VMEM((3, rank, columns), jnp.bfloat16),
            pltpu.VMEM((2, 1, length), jnp.float32),
            pltpu.VMEM((3, rows, columns), jnp.float32),
            pltpu.VMEM((3, 1, columns), jnp.float32),
            pltpu.VMEM((3, rounds + 1, 1, columns), jnp.float32),
            pltpu.SemaphoreType.DMA((4, 3)),
            pltpu.SemaphoreType.DMA((3,)),
            pltpu.SemaphoreType.DMA((3,)),
            pltpu.SemaphoreType.DMA((3, rounds)),
            pltpu.SemaphoreType.DMA((3, rounds)),
            pltpu.SemaphoreType.DMA((rounds,)),
            pltpu.SemaphoreType.DMA((rounds,)),
            pltpu.SemaphoreType.DMA((steps, 2, 2, half)),
            pltpu.SemaphoreType.DMA((3,)),
            pltpu.VMEM((3, rank, rows), jnp.bfloat16),
            pltpu.VMEM((3, 1, columns), jnp.float32),
            pltpu.VMEM((width, n, 1, length), jnp.float32),
            pltpu.SemaphoreType.DMA((4,)),
            pltpu.VMEM((n, rank, reach), jnp.bfloat16),
            pltpu.VMEM((n, reach, rank), jnp.bfloat16),
            pltpu.SemaphoreType.DMA((raw, 2, 2, half)),
            pltpu.SemaphoreType.DMA((2, half)),
            pltpu.SemaphoreType.DMA((2, half)),
            pltpu.VMEM((3, rounds, 1, columns), jnp.float32),
            pltpu.SemaphoreType.DMA((2, max(width - 1, 1))),
            pltpu.SemaphoreType.DMA((2, max(width - 1, 1))),
        ],
        compiler_params=pltpu.CompilerParams(
            collective_id=0, has_side_effects=True, vmem_limit_bytes=20 * 2**20
        ),
    )(
        w_query, w_key, w_value,
        low_query.T, low_key.T, low_value.T,
        high_query, high_key, high_value,
        norm_train.reshape(1, length), norm_step.reshape(1, length),
    )
    placed = pl.pallas_call(
        place_kernel,
        name="place",
        out_shape=[jax.ShapeDtypeStruct((n, rows, columns), jnp.bfloat16)] * 3
        + [jax.ShapeDtypeStruct((columns,), jnp.float32)] * 3
        + [jax.ShapeDtypeStruct((n * width * length,), jnp.bfloat16)],
        in_specs=[ANY] + [pl.BlockSpec(memory_space=pltpu.HBM)] * 4,
        out_specs=[ANY] * 3 + [pl.BlockSpec(memory_space=pltpu.HBM)] * 4,
        scratch_shapes=[
            pltpu.SemaphoreType.DMA((3, n)),
            *[pltpu.VMEM((1, columns), jnp.float32)] * 3,
            pltpu.VMEM((width, n, 1, length), jnp.float32),
            pltpu.SemaphoreType.DMA((8,)),
            *[pltpu.VMEM((columns,), jnp.float32)] * 3,
            pltpu.VMEM((n * width * length,), jnp.bfloat16),
        ],
        compiler_params=pltpu.CompilerParams(vmem_limit_bytes=2**20),
    )(pltpu.with_memory_space_constraint(results[0], pltpu.VMEM), *(pltpu.with_memory_space_constraint(small, pltpu.HBM) for small in results[1:]))
    return (
        *(ready.reshape(n * rows, columns) for ready in placed[0:3]),
        *placed[3:],
    )


def solution(mesh):
    n, width = mesh.shape["shard"], mesh.shape["width"]
    return jax.shard_map(
        functools.partial(body, n, width),
        mesh=mesh,
        in_specs=(
            P("shard", "width"),
            P("shard", None),
            P(None, "width"),
            P("shard", "width"),
            P("shard", None),
            P(None, "width"),
            P("shard", "width"),
            P("shard", None),
            P(None, "width"),
            P(("shard", "width")),
            P(("shard", "width")),
        ),
        out_specs=(
            P(None, "width"),
            P(None, "width"),
            P(None, "width"),
            P("width"),
            P("width"),
            P("width"),
            P(),
        ),
        check_vma=False,
    )
```

time: 187 us -> 181 us (0.968)
  Pallas kernels: 186 us -> 180 us
    pallas_call x1, Pallas kernels: 173 us -> 167 us  [body(): pl.pallas_call(functools.partial(gather_kernel, n, width), name='merge_ga...]
where the time goes in v1:
time: 181 us
  Pallas kernels  180 us (99%)
    pallas_call x1, Pallas kernels, body(): pl.pallas_call(functools.partial(gather_kernel, n, width), name='merge_ga...  167 us
    pallas_call x1, Pallas kernels, body(): pl.pallas_call(place_kernel, name='place', out_shape=[jax.ShapeDtypeStruc...  12.9 us

profile of v1, /device:TPU:0, one launch (start us, length us, event | category | flops | bytes accessed | tf_op | source)
XLA Modules:
  0.0 180.9 jit_solution(1764630219097438527)
XLA Ops:
  0.6 167.3 %merge_gather.1 = (bf16[3,8,640,1280]{3,2,1,0:T(8,128)(2,1)S(1)}, f32[1,1280]{1,0:T(1,128)}, f32[1,1280]{1,0:T(1,128)}, f32[1,1280]{1,0:T(1,128)}, f32[4,8,1,160]{3,2,1,0:T(1,128)}) custom-call(bf16[640,1280]{1,0:T(8,128)(2,1)} %refs_0_.1, bf16[640,1280]{1,0:T(8,128)(2,1)} %refs_1_.1, bf16[640,1280]{1,0:T(8,128)(2,1)} %refs_2_.1, bf16[32,640]{1,0:T(8,128)(2,1)} %bitcast.8, ...), custom_call_target="tpu_custom_call" | custom-call | tf_op jit(solution)/shard_map/merge_gather/pallas_call | solution.py:476
  168.0 12.9 %place.1 = (bf16[8,640,1280]{2,1,0:T(8,128)(2,1)}, bf16[8,640,1280]{2,1,0:T(8,128)(2,1)}, bf16[8,640,1280]{2,1,0:T(8,128)(2,1)}, f32[1280]{0:T(1024)}, f32[1280]...) custom-call(bf16[3,8,640,1280]{3,2,1,0:T(8,128)(2,1)S(1)} %get-tuple-element.19.refs_0_, ...), custom_call_target="tpu_custom_call" | custom-call | tf_op jit(solution)/shard_map/place/pallas_call | solution.py:524

commit v2 on v1

--- a/solution.py
+++ b/solution.py
@@ -8,8 +8,10 @@
 from jax.sharding import PartitionSpec as P
 
 mix_rate = 0.5
+LEAD = 1
 MESH = pl.DeviceIdType.MESH
 ANY = pl.BlockSpec(memory_space=pl.ANY)
+HBM = pl.BlockSpec(memory_space=pltpu.HBM)
 
 
 def chunks_of(rows):
@@ -23,21 +25,35 @@
     return min(2, chunks_of(rows))
 
 
+def extra_steps(rows):
+    return 3 * chunks_of(rows) // 5
+
+
+def ring_slots(half):
+    return [
+        (side, letter, hop)
+        for side in range(2)
+        for letter in range(2)
+        for hop in range(half if side == letter else half - 1)
+    ]
+
+
 def gather_kernel(n, width, *refs):
     weights, lows, highs, norms = refs[0:3], refs[3:6], refs[6:9], refs[9:11]
-    ready, small_outs = refs[11], refs[12:16]
-    w_mem, low_mem, high_mem, norm_mem, latest, scale, largest_of = refs[16:23]
-    load_sem, ring_send, pair_send, max_send, max_recv, norm_send, norm_recv = refs[23:30]
-    ring_sem, pair_sem, low_turned, held, gains, out_sem = refs[30:36]
-    low_raw, low_far, raw_send, low_send, low_recv, max_in, line_send, line_recv = refs[36:44]
-    outs = [ready.at[m] for m in range(3)]
+    ready, early, small_outs = refs[11], refs[12], refs[13:15]
+    w_mem, low_mem, high_mem, norm_mem, latest, scale, largest_of = refs[15:22]
+    load_sem, ring_send, pair_send, max_send, max_recv, norm_send, norm_recv = refs[22:29]
+    ring_sem, pair_sem, low_turned, held, gains, out_sem = refs[29:35]
+    low_raw, low_far, raw_send, low_send, low_recv, max_in, line_send, line_recv = refs[35:43]
+    outs = [ready.at[0], ready.at[1], early]
 
     rows = w_mem.shape[1]
     chips = n // 2
     half = chips // 2
     count = chunks_of(rows)
     piece = rows // (2 * count)
-    steps = 3 * count
+    shared = 2 * count
+    extra = extra_steps(rows)
     raw = raw_steps(rows)
     raw_rows = 2 * piece * raw
     reach = low_raw.shape[2]
@@ -48,6 +64,7 @@
     line = lax.axis_index("width")
     chip, core = me // 2, lax.rem(me, 2)
     sibling = me + 1 - 2 * core
+    slots = ring_slots(half)
 
     def turned(c):
         return jnp.where(c < half, c, chips + half - 1 - c)
@@ -127,7 +144,7 @@
         return pltpu.make_async_remote_copy(
             src_ref=largest_of.at[m, r],
             dst_ref=max_in.at[m, r],
-            send_sem=max_send.at[m, r],
+            send_sem=max_send.at[0],
             recv_sem=max_recv.at[m, r],
             device_id={"shard": partner(r)},
             device_id_type=MESH,
@@ -156,7 +173,7 @@
         return pltpu.make_async_remote_copy(
             src_ref=gains.at[line, pl.ds(group(r) * (1 << r), 1 << r)],
             dst_ref=gains.at[line, pl.ds(group(r) * (1 << r), 1 << r)],
-            send_sem=norm_send.at[r],
+            send_sem=norm_send.at[0],
             recv_sem=norm_recv.at[r],
             device_id={"shard": partner(r)},
             device_id_type=MESH,
@@ -172,7 +189,7 @@
         return pltpu.make_async_remote_copy(
             src_ref=block,
             dst_ref=block,
-            send_sem=line_send.at[way, s],
+            send_sem=line_send.at[way],
             recv_sem=line_recv.at[way, s],
             device_id={"width": line + sign},
             device_id_type=MESH,
@@ -231,10 +248,13 @@
     def finish(k):
         m = k // count
         at = pl.ds(rows_of(0, k), 2 * piece)
-        ready[m, me, at, :] = (latest[m, at, :] * scale[m]).astype(jnp.bfloat16)
+        outs[m][me, at, :] = (latest[m, at, :] * scale[m]).astype(jnp.bfloat16)
 
     def view(k, letter, owner):
         return outs[k // count].at[owner, pl.ds(rows_of(letter, k), piece)]
+
+    def landing(k, side, letter, hop):
+        return ring_sem.at[k % ring_sem.shape[0], slots.index((side, letter, hop))]
 
     def ring_copy(k, side, letter, hop):
         sign = 1 - 2 * side
@@ -243,11 +263,16 @@
         source = where
         if k < raw and hop == 0:
             source = w_mem.at[0, pl.ds(rows_of(letter, k), piece)]
+        sent = ring_send.at[k // count]
+        if k < raw:
+            sent = ring_send.at[3]
+            if hop > 0:
+                sent = raw_send.at[k, slots.index((side, letter, hop))]
         return pltpu.make_async_remote_copy(
             src_ref=source,
             dst_ref=where,
-            send_sem=raw_send.at[k, side, letter, hop] if k < raw else ring_send.at[k // count],
-            recv_sem=ring_sem.at[k, side, letter, hop],
+            send_sem=sent,
+            recv_sem=landing(k, side, letter, hop),
             device_id={"shard": shard_at(sign)},
             device_id_type=MESH,
         )
@@ -258,8 +283,8 @@
         return pltpu.make_async_remote_copy(
             src_ref=low_turned.at[0, :, pl.ds(0, reach)] if hop == 0 else where,
             dst_ref=where,
-            send_sem=low_send.at[side, hop],
-            recv_sem=low_recv.at[side, hop],
+            send_sem=low_send.at[0],
+            recv_sem=low_recv.at[side * half + hop],
             device_id={"shard": shard_at(sign)},
             device_id_type=MESH,
         )
@@ -271,7 +296,7 @@
         sign = 1 - 2 * side
         owner = shard_at(-sign * (hop + 1))
         where = low_raw.at[owner]
-        pltpu.make_async_copy(where, where, low_recv.at[side, hop]).wait()
+        pltpu.make_async_copy(where, where, low_recv.at[side * half + hop]).wait()
         if hop + 1 < hops(side, 0):
             low_copy(side, hop + 1).start()
         low_far[owner] = low_raw[owner].T
@@ -280,7 +305,7 @@
         sign = 1 - 2 * side
         owner = shard_at(-sign * (hop + 1))
         where = view(k, letter, owner)
-        pltpu.make_async_copy(where, where, ring_sem.at[k, side, letter, hop]).wait()
+        pltpu.make_async_copy(where, where, landing(k, side, letter, hop)).wait()
         return owner
 
     def pair_copy(k, letter, owner):
@@ -288,12 +313,29 @@
         pltpu.make_async_remote_copy(
             src_ref=where,
             dst_ref=where,
-            send_sem=pair_send.at[k // count],
-            recv_sem=pair_sem.at[k // count],
+            send_sem=pair_send.at[0],
+            recv_sem=pair_sem.at[0],
             device_id={"shard": sibling},
             device_id_type=MESH,
         ).start()
 
+    def pair_own():
+        for k in range(shared, shared + count):
+            finish(k)
+        return pltpu.make_async_remote_copy(
+            src_ref=early.at[me],
+            dst_ref=early.at[me],
+            send_sem=pair_send.at[1],
+            recv_sem=pair_sem.at[1],
+            device_id={"shard": sibling},
+            device_id_type=MESH,
+        )
+
+    def by_role(k):
+        if k < shared:
+            return lambda act: act()
+        return pl.when(core != LEAD)
+
     def hops(side, letter):
         return half if side == letter else half - 1
 
@@ -302,7 +344,7 @@
     def landed(k, side, letter, hop, owner):
         if k < raw:
             pending.append((k, side, letter, hop, owner))
-        else:
+        elif k < shared:
             pair_copy(k, letter, owner)
 
     low_seen = set()
@@ -325,41 +367,60 @@
         pending.clear()
 
     small_writes = [
-        pltpu.make_async_copy(held.at[m], small_outs[m], out_sem.at[m]) for m in range(3)
-    ] + [pltpu.make_async_copy(gains, small_outs[3], out_sem.at[3])]
+        pltpu.make_async_copy(held, small_outs[0], out_sem.at[0]),
+        pltpu.make_async_copy(gains, small_outs[1], out_sem.at[1]),
+    ]
     first.wait()
     pl.semaphore_wait(
         barrier,
         2 + rounds + (line > 0).astype(jnp.int32) + (line < width - 1).astype(jnp.int32),
     )
 
-    for j in range(steps + half + 1):
-        if j < steps:
-            for side in range(2):
-                if hops(side, side) > 0:
-                    ring_start(j, side, side, 0)
+    own_value = []
+
+    for j in range(shared + extra + half + 1):
+        if j < shared + extra:
+
+            @by_role(j)
+            def _():
+                for side in range(2):
+                    if hops(side, side) > 0:
+                        ring_start(j, side, side, 0)
+
         if j == 1:
             merge(1)
             advance(0)
-        for hop in range(half):
-            k = j - 1 - hop
-            if 0 <= k < steps and hop + 1 < half:
-                for side in range(2):
-                    owner = ring_arrival(k, side, side, hop)
-                    ring_start(k, side, side, hop + 1)
-                    landed(k, side, side, hop, owner)
-        if j < steps:
-            for side in range(2):
-                if hops(side, 1 - side) > 0:
-                    ring_start(j, side, 1 - side, 0)
         for hop in range(half - 1):
             k = j - 1 - hop
-            if 0 <= k < steps and hop + 1 < half - 1:
+            if 0 <= k < shared + extra:
+
+                @by_role(k)
+                def _():
+                    for side in range(2):
+                        owner = ring_arrival(k, side, side, hop)
+                        ring_start(k, side, side, hop + 1)
+                        landed(k, side, side, hop, owner)
+
+        if j < shared + extra:
+
+            @by_role(j)
+            def _():
                 for side in range(2):
-                    owner = ring_arrival(k, side, 1 - side, hop)
-                    ring_start(k, side, 1 - side, hop + 1)
-                    landed(k, side, 1 - side, hop, owner)
-        if raw <= j < steps:
+                    if hops(side, 1 - side) > 0:
+                        ring_start(j, side, 1 - side, 0)
+
+        for hop in range(half - 2):
+            k = j - 1 - hop
+            if 0 <= k < shared + extra:
+
+                @by_role(k)
+                def _():
+                    for side in range(2):
+                        owner = ring_arrival(k, side, 1 - side, hop)
+                        ring_start(k, side, 1 - side, hop + 1)
+                        landed(k, side, 1 - side, hop, owner)
+
+        if raw <= j < shared:
             for letter in range(2):
                 pair_copy(j, letter, me)
         if j == 0:
@@ -380,12 +441,16 @@
                     low_arrival(side, j - 1)
         if j > 0 and errands:
             errands.pop(0)()
-        if j == steps - 1:
+        if j == min(raw + rounds + 2, shared - 1):
+            settle(2)
+            own_value.append(pair_own())
+            own_value[0].start()
+        if j == shared - 1:
             while errands:
                 errands.pop(0)()
             for copy in small_writes:
                 copy.start()
-        if raw <= j + 1 < steps:
+        if raw <= j + 1 < shared:
             if j + 1 == raw:
                 settle(0)
             if (j + 1) % count == 0:
@@ -395,9 +460,13 @@
             for letter in (side, 1 - side):
                 hop = hops(side, letter) - 1
                 k = j - 2 - hop
-                if hop >= 0 and 0 <= k < steps:
-                    owner = ring_arrival(k, side, letter, hop)
-                    landed(k, side, letter, hop, owner)
+                if hop >= 0 and 0 <= k < shared + extra:
+
+                    @by_role(k)
+                    def _():
+                        owner = ring_arrival(k, side, letter, hop)
+                        landed(k, side, letter, hop, owner)
+
         if j == raw:
             for k in range(raw):
                 finish(k)
@@ -406,62 +475,235 @@
         if j >= raw:
             absorb()
 
-    for m in range(3):
-        theirs = outs[m].at[pl.ds(0, chips)]
-        pltpu.make_async_copy(theirs, theirs, pair_sem.at[m]).wait()
-        pltpu.make_async_copy(theirs, theirs, pair_send.at[m]).wait()
+    theirs = ready.at[:, pl.ds(0, chips)]
+    pltpu.make_async_copy(theirs, theirs, pair_sem.at[0]).wait()
+    pltpu.make_async_copy(theirs, theirs, pair_send.at[0]).wait()
+    pltpu.make_async_copy(early.at[sibling], early.at[sibling], pair_sem.at[1]).wait()
+    own_value[0].wait_send()
+    for m in range(2):
         kept = raw_rows if m == 0 else 0
         if kept < rows:
             sent = outs[m].at[pl.ds(0, chips - 1), pl.ds(kept, rows - kept)]
             pltpu.make_async_copy(sent, sent, ring_send.at[m]).wait()
-        for r in range(rounds):
-            max_copy(m, r).wait_send()
-    for side in range(2):
-        for k in range(raw):
-            for letter in range(2):
-                if hops(side, letter) > 0:
-                    ring_copy(k, side, letter, 0).wait_send()
-        for hop in range(hops(side, 0)):
-            low_copy(side, hop).wait_send()
-    for r in range(rounds):
-        gain_copy(r).wait_send()
+    sent = ready.at[0, pl.ds(0, len([s for s in slots if s[2] == 0]) // 2), pl.ds(0, raw_rows)]
+    pltpu.make_async_copy(sent, sent, ring_send.at[3]).wait()
+    if extra > 0:
+
+        @pl.when(core != LEAD)
+        def _():
+            sent = early.at[pl.ds(0, chips - 1), pl.ds(0, 2 * piece * extra)]
+            pltpu.make_async_copy(sent, sent, ring_send.at[2]).wait()
+
+    pltpu.make_async_copy(max_in, max_in, max_send.at[0]).wait()
+    sent = low_raw.at[pl.ds(0, chips - 1)]
+    pltpu.make_async_copy(sent, sent, low_send.at[0]).wait()
+    sent = gains.at[line, pl.ds(0, n - 1)]
+    pltpu.make_async_copy(sent, sent, norm_send.at[0]).wait()
     for copy in small_writes:
         copy.wait()
 
 
-def place_kernel(*refs):
-    source, small = refs[0], refs[1:5]
-    targets, finals, sem = refs[5:8], refs[8:12], refs[12]
-    factors, gains, small_sem = refs[13:16], refs[16], refs[17]
-    scales, serve = refs[18:21], refs[21]
+def late_kernel(n, *refs):
+    early, late = refs[0], refs[2]
+    ring_send, pair_send, pair_sem, ring_sem, joined = refs[3:8]
+    rows = early.shape[1]
+    chips = n // 2
+    half = chips // 2
+    count = chunks_of(rows)
+    piece = rows // (2 * count)
+    extra = extra_steps(rows)
+    early_rows = 2 * piece * extra
+    slots = ring_slots(half)
+
+    me = lax.axis_index("shard")
+    chip, core = me // 2, lax.rem(me, 2)
+    sibling = me + 1 - 2 * core
+
+    def turned(c):
+        return jnp.where(c < half, c, chips + half - 1 - c)
+
+    place = turned(chip)
+
+    def shard_at(offset):
+        return turned(lax.rem(place + offset + 2 * chips, chips)) * 2 + core
+
+    def hops(side, letter):
+        return half if side == letter else half - 1
+
+    def view(ref, k, letter, owner):
+        return ref.at[owner, pl.ds((2 * k + letter) * piece, piece)]
+
+    def ring_copy(k, side, letter, hop):
+        sign = 1 - 2 * side
+        owner = shard_at(-sign * hop)
+        return pltpu.make_async_remote_copy(
+            src_ref=view(early if hop == 0 else late, k, letter, owner),
+            dst_ref=view(late, k, letter, owner),
+            send_sem=ring_send.at[0],
+            recv_sem=ring_sem.at[k, slots.index((side, letter, hop))],
+            device_id={"shard": shard_at(sign)},
+            device_id_type=MESH,
+        )
+
+    def ring_arrival(k, side, letter, hop):
+        sign = 1 - 2 * side
+        owner = shard_at(-sign * (hop + 1))
+        where = view(late, k, letter, owner)
+        landed = ring_sem.at[k, slots.index((side, letter, hop))]
+        pltpu.make_async_copy(where, where, landed).wait()
+        return owner
+
+    def to_sibling(source, target):
+        pltpu.make_async_remote_copy(
+            src_ref=source,
+            dst_ref=target,
+            send_sem=pair_send.at[0],
+            recv_sem=pair_sem.at[0],
+            device_id={"shard": sibling},
+            device_id_type=MESH,
+        ).start()
+
+    barrier = pltpu.get_barrier_semaphore()
+    for offset in (1, -1):
+        pl.semaphore_signal(
+            barrier, inc=1, device_id={"shard": shard_at(offset)}, device_id_type=MESH
+        )
+
+    def run(first, join):
+        waiting = []
+
+        def landed(k, letter, owner):
+            where = view(late, k, letter, owner)
+            if join is not None and not joined_at:
+                waiting.append(where)
+            else:
+                to_sibling(where, where)
+
+        joined_at = []
+        for j in range(first, count + half + 1):
+            if j < count:
+                for side in range(2):
+                    if hops(side, side) > 0:
+                        ring_copy(j, side, side, 0).start()
+            for hop in range(half - 1):
+                k = j - 1 - hop
+                if first <= k < count:
+                    for side in range(2):
+                        owner = ring_arrival(k, side, side, hop)
+                        ring_copy(k, side, side, hop + 1).start()
+                        landed(k, side, owner)
+            if j < count:
+                for side in range(2):
+                    if hops(side, 1 - side) > 0:
+                        ring_copy(j, side, 1 - side, 0).start()
+            for hop in range(half - 2):
+                k = j - 1 - hop
+                if first <= k < count:
+                    for side in range(2):
+                        owner = ring_arrival(k, side, 1 - side, hop)
+                        ring_copy(k, side, 1 - side, hop + 1).start()
+                        landed(k, 1 - side, owner)
+            if j == join:
+                pl.semaphore_wait(joined, 1)
+                joined_at.append(j)
+                for where in waiting:
+                    to_sibling(where, where)
+            for side in range(2):
+                for letter in (side, 1 - side):
+                    hop = hops(side, letter) - 1
+                    k = j - 2 - hop
+                    if hop >= 0 and first <= k < count:
+                        landed(k, letter, ring_arrival(k, side, letter, hop))
+        sent = late.at[pl.ds(0, chips - 1), pl.ds(0, 2 * piece * (count - first))]
+        pltpu.make_async_copy(sent, sent, ring_send.at[0]).wait()
+
+    @pl.when(core == LEAD)
+    def _():
+        pl.semaphore_signal(barrier, inc=1, device_id={"shard": sibling}, device_id_type=MESH)
+        pl.semaphore_wait(barrier, 2)
+        run(0, min(extra + 1, count - 1))
+
+    @pl.when(core != LEAD)
+    def _():
+        pl.semaphore_wait(barrier, 3)
+        pl.semaphore_signal(joined, inc=1, device_id={"shard": sibling}, device_id_type=MESH)
+        if extra > 0:
+            for offset in range(1, chips):
+                owner = shard_at(offset)
+                at = pl.ds(0, early_rows)
+                to_sibling(early.at[owner, at], late.at[owner, at])
+        run(extra, None)
+
+    theirs = late.at[pl.ds(0, chips - 1)]
+    pltpu.make_async_copy(theirs, theirs, pair_sem.at[0]).wait()
+    pltpu.make_async_copy(theirs, theirs, pair_send.at[0]).wait()
+
+
+def place_first(*refs):
+    source, small = refs[0], refs[1:3]
+    targets, finals, sem = refs[3:5], refs[5:9], refs[9]
+    factors, gains, small_sem = refs[10], refs[11], refs[12]
+    scales, serve = refs[13:16], refs[16]
     writes = [
-        pltpu.make_async_copy(refs[18 + i], finals[i], small_sem.at[4 + i]) for i in range(4)
+        pltpu.make_async_copy(refs[13 + i], finals[i], small_sem.at[2 + i]) for i in range(4)
     ]
     loads = [
-        pltpu.make_async_copy(small[i], refs[13 + i], small_sem.at[i]) for i in range(4)
+        pltpu.make_async_copy(small[i], refs[10 + i], small_sem.at[i]) for i in range(2)
     ]
-    for copy in loads:
-        copy.start()
-    copies = []
-    for m in range(3):
-        for i in range(source.shape[1]):
-            copies.append(
-                pltpu.make_async_copy(source.at[m, i], targets[m].at[i], sem.at[m, i])
-            )
-    for copy in copies:
+    copies = [
+        pltpu.make_async_copy(source.at[m, i], targets[m].at[i], sem.at[2 if m else min(i, 1)])
+        for m in range(2)
+        for i in range(source.shape[1])
+    ]
+    for copy in loads + copies:
         copy.start()
     for copy in loads:
         copy.wait()
     for m in range(3):
-        scales[m][...] = factors[m][...].reshape(scales[m].shape)
+        scales[m][...] = factors[m].reshape(scales[m].shape)
     blocks = [gains[k, i] for i in range(gains.shape[1]) for k in range(gains.shape[0])]
     line = jnp.concatenate(blocks, axis=1)
     serve[...] = line.reshape(serve.shape).astype(jnp.bfloat16)
     copies[0].wait()
     for copy in writes:
         copy.start()
-    for copy in copies[1:] + writes:
+    rest = source.at[0, pl.ds(1, source.shape[1] - 1)]
+    both = source.at[1]
+    pltpu.make_async_copy(rest, rest, sem.at[1]).wait()
+    pltpu.make_async_copy(both, both, sem.at[2]).wait()
+    for copy in writes:
         copy.wait()
+
+
+def place_last(*refs):
+    early, late, target, sem = refs
+    n, rows = early.shape[0], early.shape[1]
+    chips = n // 2
+    early_rows = 2 * (rows // (2 * chunks_of(rows))) * extra_steps(rows)
+    me = lax.axis_index("shard")
+    chip, core = me // 2, lax.rem(me, 2)
+
+    def put(source, owner, *at):
+        where = (owner, *at)
+        pltpu.make_async_copy(source.at[where], target.at[where], sem.at[0]).start()
+
+    put(early, me)
+    put(early, me + 1 - 2 * core)
+    for offset in range(1, chips):
+        other = lax.rem(chip + offset, chips) * 2
+        put(late, other + 1 - core)
+
+        @pl.when(core == LEAD)
+        def _():
+            put(late, other + core)
+
+        @pl.when(core != LEAD)
+        def _():
+            if early_rows > 0:
+                put(early, other + core, pl.ds(0, early_rows))
+            put(late, other + core, pl.ds(early_rows, rows - early_rows))
+
+    pltpu.make_async_copy(late, late, sem.at[0]).wait()
 
 
 def body(n, width, w_query, low_query, high_query, w_key, low_key, high_key, w_value, low_value, high_value, norm_train, norm_step):
@@ -469,19 +711,30 @@
     rank = low_query.shape[1]
     length = norm_train.shape[0]
     half = n // 4
-    steps = 3 * chunks_of(rows)
+    count = chunks_of(rows)
     raw = raw_steps(rows)
     rounds = n.bit_length() - 1
-    reach = min(rows, -(-(rows // chunks_of(rows)) * raw // 128) * 128)
-    results = pl.pallas_call(
+    reach = min(rows, -(-(rows // count) * raw // 128) * 128)
+    slots = len(ring_slots(half))
+    block = jax.ShapeDtypeStruct((n, rows, columns), jnp.bfloat16)
+
+    def near(value):
+        return pltpu.with_memory_space_constraint(value, pltpu.VMEM)
+
+    def far(value):
+        return pltpu.with_memory_space_constraint(value, pltpu.HBM)
+
+    ready, early, factors, gains = pl.pallas_call(
         functools.partial(gather_kernel, n, width),
         name="merge_gather",
-        out_shape=[pltpu.VMEM((3, n, rows, columns), jnp.bfloat16)]
-        + [jax.ShapeDtypeStruct((1, columns), jnp.float32)] * 3
-        + [jax.ShapeDtypeStruct((width, n, 1, length), jnp.float32)],
+        out_shape=[
+            pltpu.VMEM((2, n, rows, columns), jnp.bfloat16),
+            pltpu.VMEM((n, rows, columns), jnp.bfloat16),
+            jax.ShapeDtypeStruct((3, 1, columns), jnp.float32),
+            jax.ShapeDtypeStruct((width, n, 1, length), jnp.float32),
+        ],
         in_specs=[ANY] * 11,
-        out_specs=[pl.BlockSpec(memory_space=pltpu.VMEM)]
-        + [pl.BlockSpec(memory_space=pltpu.HBM)] * 4,
+        out_specs=[pl.BlockSpec(memory_space=pltpu.VMEM)] * 2 + [HBM] * 2,
         scratch_shapes=[
             pltpu.VMEM((3, rows, columns), jnp.bfloat16),
             pltpu.VMEM((3, rows, rank), jnp.bfloat16),
@@ -491,25 +744,25 @@
             pltpu.VMEM((3, 1, columns), jnp.float32),
             pltpu.VMEM((3, rounds + 1, 1, columns), jnp.float32),
             pltpu.SemaphoreType.DMA((4, 3)),
-            pltpu.SemaphoreType.DMA((3,)),
-            pltpu.SemaphoreType.DMA((3,)),
+            pltpu.SemaphoreType.DMA((4,)),
+            pltpu.SemaphoreType.DMA((2,)),
+            pltpu.SemaphoreType.DMA((1,)),
             pltpu.SemaphoreType.DMA((3, rounds)),
-            pltpu.SemaphoreType.DMA((3, rounds)),
+            pltpu.SemaphoreType.DMA((1,)),
             pltpu.SemaphoreType.DMA((rounds,)),
-            pltpu.SemaphoreType.DMA((rounds,)),
-            pltpu.SemaphoreType.DMA((steps, 2, 2, half)),
-            pltpu.SemaphoreType.DMA((3,)),
+            pltpu.SemaphoreType.DMA((5, slots)),
+            pltpu.SemaphoreType.DMA((2,)),
             pltpu.VMEM((3, rank, rows), jnp.bfloat16),
             pltpu.VMEM((3, 1, columns), jnp.float32),
             pltpu.VMEM((width, n, 1, length), jnp.float32),
-            pltpu.SemaphoreType.DMA((4,)),
+            pltpu.SemaphoreType.DMA((2,)),
             pltpu.VMEM((n, rank, reach), jnp.bfloat16),
             pltpu.VMEM((n, reach, rank), jnp.bfloat16),
-            pltpu.SemaphoreType.DMA((raw, 2, 2, half)),
-            pltpu.SemaphoreType.DMA((2, half)),
-            pltpu.SemaphoreType.DMA((2, half)),
+            pltpu.SemaphoreType.DMA((raw, slots)),
+            pltpu.SemaphoreType.DMA((1,)),
+            pltpu.SemaphoreType.DMA((2 * half,)),
             pltpu.VMEM((3, rounds, 1, columns), jnp.float32),
-            pltpu.SemaphoreType.DMA((2, max(width - 1, 1))),
+            pltpu.SemaphoreType.DMA((2,)),
             pltpu.SemaphoreType.DMA((2, max(width - 1, 1))),
         ],
         compiler_params=pltpu.CompilerParams(
@@ -521,27 +774,53 @@
         high_query, high_key, high_value,
         norm_train.reshape(1, length), norm_step.reshape(1, length),
     )
-    placed = pl.pallas_call(
-        place_kernel,
-        name="place",
-        out_shape=[jax.ShapeDtypeStruct((n, rows, columns), jnp.bfloat16)] * 3
+    query, key, *small = pl.pallas_call(
+        place_first,
+        name="place_first",
+        out_shape=[block] * 2
         + [jax.ShapeDtypeStruct((columns,), jnp.float32)] * 3
         + [jax.ShapeDtypeStruct((n * width * length,), jnp.bfloat16)],
-        in_specs=[ANY] + [pl.BlockSpec(memory_space=pltpu.HBM)] * 4,
-        out_specs=[ANY] * 3 + [pl.BlockSpec(memory_space=pltpu.HBM)] * 4,
+        in_specs=[ANY] + [HBM] * 2,
+        out_specs=[HBM] * 6,
         scratch_shapes=[
-            pltpu.SemaphoreType.DMA((3, n)),
-            *[pltpu.VMEM((1, columns), jnp.float32)] * 3,
+            pltpu.SemaphoreType.DMA((3,)),
+            pltpu.VMEM((3, 1, columns), jnp.float32),
             pltpu.VMEM((width, n, 1, length), jnp.float32),
-            pltpu.SemaphoreType.DMA((8,)),
+            pltpu.SemaphoreType.DMA((6,)),
             *[pltpu.VMEM((columns,), jnp.float32)] * 3,
             pltpu.VMEM((n * width * length,), jnp.bfloat16),
         ],
         compiler_params=pltpu.CompilerParams(vmem_limit_bytes=2**20),
-    )(pltpu.with_memory_space_constraint(results[0], pltpu.VMEM), *(pltpu.with_memory_space_constraint(small, pltpu.HBM) for small in results[1:]))
+    )(near(ready), far(factors), far(gains))
+    late = pl.pallas_call(
+        functools.partial(late_kernel, n),
+        name="gather_late",
+        out_shape=pltpu.VMEM((n, rows, columns), jnp.bfloat16),
+        in_specs=[ANY, HBM],
+        out_specs=pl.BlockSpec(memory_space=pltpu.VMEM),
+        scratch_shapes=[
+            pltpu.SemaphoreType.DMA((1,)),
+            pltpu.SemaphoreType.DMA((1,)),
+            pltpu.SemaphoreType.DMA((1,)),
+            pltpu.SemaphoreType.DMA((count, slots)),
+            pltpu.SemaphoreType.REGULAR,
+        ],
+        compiler_params=pltpu.CompilerParams(
+            collective_id=1, has_side_effects=True, vmem_limit_bytes=2**20
+        ),
+    )(near(early), far(small[0]))
+    value = pl.pallas_call(
+        place_last,
+        name="place_last",
+        out_shape=block,
+        in_specs=[ANY] * 2,
+        out_specs=HBM,
+        scratch_shapes=[pltpu.SemaphoreType.DMA((1,))],
+        compiler_params=pltpu.CompilerParams(vmem_limit_bytes=2**20),
+    )(near(early), near(late))
     return (
-        *(ready.reshape(n * rows, columns) for ready in placed[0:3]),
-        *placed[3:],
+        *(ready.reshape(n * rows, columns) for ready in (query, key, value)),
+        *small,
     )
 
 

time: 181 us -> 174 us (0.961)
  Pallas kernels: 180 us -> 174 us
    pallas_call x1, Pallas kernels: 167 us -> 128 us  [body(): pl.pallas_call(functools.partial(gather_kernel, n, width), name='merge_ga...]
    pallas_call x1 -> x3, Pallas kernels: 12.9 us -> 45.4 us  [the longest x1 31.9 us: body(): pl.pallas_call(functools.partial(late_kernel, n), name='gather_late', out...]
where the time goes in v2:
time: 174 us
  Pallas kernels  174 us (100%)
    pallas_call x1, Pallas kernels, body(): pl.pallas_call(functools.partial(gather_kernel, n, width), name='merge_ga...  128 us
    pallas_call x1, Pallas kernels, body(): pl.pallas_call(functools.partial(late_kernel, n), name='gather_late', out...  31.9 us
    pallas_call x1, Pallas kernels, body(): pl.pallas_call(place_first, name='place_first', out_shape=[block] * 2 + [...  8.78 us
    pallas_call x1, Pallas kernels, body(): pl.pallas_call(place_last, name='place_last', out_shape=block, in_specs=[...  4.74 us

profile of v2, /device:TPU:0, one launch (start us, length us, event | category | flops | bytes accessed | tf_op | source)
XLA Modules:
  0.0 174.2 jit_solution(9055706873553886481)
XLA Ops:
  0.6 128.2 %merge_gather.1 = (bf16[2,8,640,1280]{3,2,1,0:T(8,128)(2,1)S(1)}, bf16[8,640,1280]{2,1,0:T(8,128)(2,1)S(1)}, f32[3,1,1280]{2,1,0:T(1,128)}, f32[4,8,1,160]{3,2,1,0:T(1,128)}) custom-call(bf16[640,1280]{1,0:T(8,128)(2,1)} %refs_0_.1, bf16[640,1280]{1,0:T(8,128)(2,1)} %refs_1_.1, bf16[640,1280]{1,0:T(8,128)(2,1)} %refs_2_.1, bf16[32,640]{1,0:T(8,128)(2,1)} %bitcast.9, ...), custom_call_target="tpu_custom_call" | custom-call | tf_op jit(solution)/shard_map/merge_gather/pallas_call | solution.py:727
  128.8 8.8 %place_first.1 = (bf16[8,640,1280]{2,1,0:T(8,128)(2,1)}, bf16[8,640,1280]{2,1,0:T(8,128)(2,1)}, f32[1280]{0:T(1024)}, f32[1280]{0:T(1024)}, f32[1280]{0:T(1024)}, /*index=5*/bf16[5120]{0:T(1024)(128)(2,1)}) custom-call(bf16[2,8,640,1280]{3,2,1,0:T(8,128)(2,1)S(1)} %get-tuple-element.17.refs_0_, f32[3,1,1280]{2,1,0:T(1,128)} %get-tuple-element.18.refs_1_, ...), custom_call_target="tpu_custom_call" | custom-call | tf_op jit(solution)/shard_map/place_first/pallas_call | solution.py:777
  137.6 31.9 %gather_late.1.refs_1_ = bf16[8,640,1280]{2,1,0:T(8,128)(2,1)S(1)} custom-call(bf16[8,640,1280]{2,1,0:T(8,128)(2,1)S(1)} %get-tuple-element.22.refs_0_, f32[1280]{0:T(1024)} %get-tuple-element.13.refs_1_), custom_call_target="tpu_custom_call" | custom-call | tf_op jit(solution)/shard_map/gather_late/pallas_call | solution.py:795
  169.5 4.7 %place_last.1 = bf16[8,640,1280]{2,1,0:T(8,128)(2,1)} custom-call(bf16[8,640,1280]{2,1,0:T(8,128)(2,1)S(1)} %get-tuple-element.22.refs_0_, bf16[8,640,1280]{2,1,0:T(8,128)(2,1)S(1)} %gather_late.1.refs_1_), custom_call_target="tpu_custom_call" | custom-call | tf_op jit(solution)/shard_map/place_last/pallas_call | solution.py:812

commit v3 on v2

--- a/solution.py
+++ b/solution.py
@@ -9,6 +9,7 @@
 
 mix_rate = 0.5
 LEAD = 1
+BOTH = 1
 MESH = pl.DeviceIdType.MESH
 ANY = pl.BlockSpec(memory_space=pl.ANY)
 HBM = pl.BlockSpec(memory_space=pltpu.HBM)
@@ -25,8 +26,10 @@
     return min(2, chunks_of(rows))
 
 
-def extra_steps(rows):
-    return 3 * chunks_of(rows) // 5
+def value_split(rows):
+    count = chunks_of(rows)
+    extra = 3 * count // 5
+    return min(count // 5 * BOTH, count - extra), extra
 
 
 def ring_slots(half):
@@ -52,8 +55,9 @@
     half = chips // 2
     count = chunks_of(rows)
     piece = rows // (2 * count)
-    shared = 2 * count
-    extra = extra_steps(rows)
+    both, extra = value_split(rows)
+    shared = 2 * count + both
+    both_rows = 2 * piece * both
     raw = raw_steps(rows)
     raw_rows = 2 * piece * raw
     reach = low_raw.shape[2]
@@ -313,14 +317,14 @@
         pltpu.make_async_remote_copy(
             src_ref=where,
             dst_ref=where,
-            send_sem=pair_send.at[0],
-            recv_sem=pair_sem.at[0],
+            send_sem=pair_send.at[k // (2 * count) * 2],
+            recv_sem=pair_sem.at[k // (2 * count) * 2],
             device_id={"shard": sibling},
             device_id_type=MESH,
         ).start()
 
     def pair_own():
-        for k in range(shared, shared + count):
+        for k in range(2 * count, 3 * count):
             finish(k)
         return pltpu.make_async_remote_copy(
             src_ref=early.at[me],
@@ -377,16 +381,21 @@
     )
 
     own_value = []
-
-    for j in range(shared + extra + half + 1):
-        if j < shared + extra:
-
-            @by_role(j)
-            def _():
-                for side in range(2):
-                    if hops(side, side) > 0:
-                        ring_start(j, side, side, 0)
-
+    closed = set()
+    last_hops = [s for side in range(2) for s in slots[::-1] if s[0] == side and s[2] == hops(*s[0:2]) - 1]
+
+    def close(k, side, letter, hop):
+        closed.add((k, side, letter))
+        landed(k, side, letter, hop, ring_arrival(k, side, letter, hop))
+
+    for j in range(shared + extra + half):
+        def first_own():
+            for side in range(2):
+                if hops(side, side) > 0:
+                    ring_start(j, side, side, 0)
+
+        if j < shared + extra and j != shared:
+            by_role(j)(first_own)
         if j == 1:
             merge(1)
             advance(0)
@@ -401,6 +410,8 @@
                         ring_start(k, side, side, hop + 1)
                         landed(k, side, side, hop, owner)
 
+        if j == shared and extra > 0:
+            by_role(j)(first_own)
         if j < shared + extra:
 
             @by_role(j)
@@ -420,7 +431,7 @@
                         ring_start(k, side, 1 - side, hop + 1)
                         landed(k, side, 1 - side, hop, owner)
 
-        if raw <= j < shared:
+        if raw <= j < 2 * count:
             for letter in range(2):
                 pair_copy(j, letter, me)
         if j == 0:
@@ -441,32 +452,28 @@
                     low_arrival(side, j - 1)
         if j > 0 and errands:
             errands.pop(0)()
-        if j == min(raw + rounds + 2, shared - 1):
+        if j == min(raw + rounds + 2, 2 * count - 1):
             settle(2)
             own_value.append(pair_own())
             own_value[0].start()
-        if j == shared - 1:
+        if j == 2 * count - 1:
             while errands:
                 errands.pop(0)()
             for copy in small_writes:
                 copy.start()
-        if raw <= j + 1 < shared:
+        if raw <= j + 1 < 2 * count:
             if j + 1 == raw:
                 settle(0)
             if (j + 1) % count == 0:
                 settle((j + 1) // count)
             finish(j + 1)
-        for side in range(2):
-            for letter in (side, 1 - side):
-                hop = hops(side, letter) - 1
-                k = j - 2 - hop
-                if hop >= 0 and 0 <= k < shared + extra:
-
-                    @by_role(k)
-                    def _():
-                        owner = ring_arrival(k, side, letter, hop)
-                        landed(k, side, letter, hop, owner)
-
+        for side, letter, hop in last_hops:
+            k = j - 1 - hop
+            if 0 <= k < shared + extra and (k, side, letter) not in closed:
+                by_role(k)(functools.partial(close, k, side, letter, hop))
+        if j == shared and half == 2:
+            for side in range(2):
+                close(shared - 1, side, side, half - 1)
         if j == raw:
             for k in range(raw):
                 finish(k)
@@ -480,6 +487,14 @@
     pltpu.make_async_copy(theirs, theirs, pair_send.at[0]).wait()
     pltpu.make_async_copy(early.at[sibling], early.at[sibling], pair_sem.at[1]).wait()
     own_value[0].wait_send()
+
+    def value_part(share):
+        return early.at[pl.ds(0, chips - 1), pl.ds(0, share * 2 * piece)]
+
+    if both > 0:
+        theirs = value_part(both)
+        pltpu.make_async_copy(theirs, theirs, pair_sem.at[2]).wait()
+        pltpu.make_async_copy(theirs, theirs, pair_send.at[2]).wait()
     for m in range(2):
         kept = raw_rows if m == 0 else 0
         if kept < rows:
@@ -487,12 +502,13 @@
             pltpu.make_async_copy(sent, sent, ring_send.at[m]).wait()
     sent = ready.at[0, pl.ds(0, len([s for s in slots if s[2] == 0]) // 2), pl.ds(0, raw_rows)]
     pltpu.make_async_copy(sent, sent, ring_send.at[3]).wait()
-    if extra > 0:
-
-        @pl.when(core != LEAD)
-        def _():
-            sent = early.at[pl.ds(0, chips - 1), pl.ds(0, 2 * piece * extra)]
-            pltpu.make_async_copy(sent, sent, ring_send.at[2]).wait()
+    for share, mine in ((both, core == LEAD), (both + extra, core != LEAD)):
+        if share > 0:
+
+            @pl.when(mine)
+            def _():
+                sent = value_part(share)
+                pltpu.make_async_copy(sent, sent, ring_send.at[2]).wait()
 
     pltpu.make_async_copy(max_in, max_in, max_send.at[0]).wait()
     sent = low_raw.at[pl.ds(0, chips - 1)]
@@ -511,8 +527,7 @@
     half = chips // 2
     count = chunks_of(rows)
     piece = rows // (2 * count)
-    extra = extra_steps(rows)
-    early_rows = 2 * piece * extra
+    both, extra = value_split(rows)
     slots = ring_slots(half)
 
     me = lax.axis_index("shard")
@@ -580,7 +595,7 @@
                 to_sibling(where, where)
 
         joined_at = []
-        for j in range(first, count + half + 1):
+        for j in range(first, count + half):
             if j < count:
                 for side in range(2):
                     if hops(side, side) > 0:
@@ -611,17 +626,18 @@
             for side in range(2):
                 for letter in (side, 1 - side):
                     hop = hops(side, letter) - 1
-                    k = j - 2 - hop
+                    k = j - 1 - hop
                     if hop >= 0 and first <= k < count:
                         landed(k, letter, ring_arrival(k, side, letter, hop))
-        sent = late.at[pl.ds(0, chips - 1), pl.ds(0, 2 * piece * (count - first))]
-        pltpu.make_async_copy(sent, sent, ring_send.at[0]).wait()
+        if first < count:
+            sent = late.at[pl.ds(0, chips - 1), pl.ds(0, 2 * piece * (count - first))]
+            pltpu.make_async_copy(sent, sent, ring_send.at[0]).wait()
 
     @pl.when(core == LEAD)
     def _():
         pl.semaphore_signal(barrier, inc=1, device_id={"shard": sibling}, device_id_type=MESH)
         pl.semaphore_wait(barrier, 2)
-        run(0, min(extra + 1, count - 1))
+        run(both, count - 1 if both + extra < count else count)
 
     @pl.when(core != LEAD)
     def _():
@@ -630,26 +646,29 @@
         if extra > 0:
             for offset in range(1, chips):
                 owner = shard_at(offset)
-                at = pl.ds(0, early_rows)
+                at = pl.ds(2 * piece * both, 2 * piece * extra)
                 to_sibling(early.at[owner, at], late.at[owner, at])
-        run(extra, None)
-
-    theirs = late.at[pl.ds(0, chips - 1)]
+        run(both + extra, None)
+
+    theirs = late.at[pl.ds(0, chips - 1), pl.ds(0, 2 * piece * (count - both))]
     pltpu.make_async_copy(theirs, theirs, pair_sem.at[0]).wait()
     pltpu.make_async_copy(theirs, theirs, pair_send.at[0]).wait()
 
 
 def place_first(*refs):
-    source, small = refs[0], refs[1:3]
-    targets, finals, sem = refs[3:5], refs[5:9], refs[9]
-    factors, gains, small_sem = refs[10], refs[11], refs[12]
-    scales, serve = refs[13:16], refs[16]
+    source, early, small = refs[0], refs[1], refs[2:4]
+    targets, finals, sem = refs[4:7], refs[7:11], refs[11]
+    factors, gains, small_sem = refs[12], refs[13], refs[14]
+    scales, serve = refs[15:18], refs[18]
     writes = [
-        pltpu.make_async_copy(refs[13 + i], finals[i], small_sem.at[2 + i]) for i in range(4)
+        pltpu.make_async_copy(refs[15 + i], finals[i], small_sem.at[2 + i]) for i in range(4)
     ]
     loads = [
-        pltpu.make_async_copy(small[i], refs[10 + i], small_sem.at[i]) for i in range(2)
+        pltpu.make_async_copy(small[i], refs[12 + i], small_sem.at[i]) for i in range(2)
     ]
+    n, rows = early.shape[0], early.shape[1]
+    both_rows = rows // chunks_of(rows) * value_split(rows)[0]
+    chip = lax.div(lax.axis_index("shard"), 2)
     copies = [
         pltpu.make_async_copy(source.at[m, i], targets[m].at[i], sem.at[2 if m else min(i, 1)])
         for m in range(2)
@@ -657,6 +676,12 @@
     ]
     for copy in loads + copies:
         copy.start()
+    ours = pl.ds(2 * chip, 2)
+    pltpu.make_async_copy(early.at[ours], targets[2].at[ours], sem.at[3]).start()
+    if both_rows > 0:
+        for offset in range(1, n // 2):
+            where = pl.ds(2 * lax.rem(chip + offset, n // 2), 2), pl.ds(0, both_rows)
+            pltpu.make_async_copy(early.at[where], targets[2].at[where], sem.at[4]).start()
     for copy in loads:
         copy.wait()
     for m in range(3):
@@ -671,39 +696,43 @@
     both = source.at[1]
     pltpu.make_async_copy(rest, rest, sem.at[1]).wait()
     pltpu.make_async_copy(both, both, sem.at[2]).wait()
+    pltpu.make_async_copy(early.at[ours], targets[2].at[ours], sem.at[3]).wait()
+    if both_rows > 0:
+        part = early.at[pl.ds(0, n - 2), pl.ds(0, both_rows)]
+        pltpu.make_async_copy(part, part, sem.at[4]).wait()
     for copy in writes:
         copy.wait()
 
 
-def place_last(*refs):
-    early, late, target, sem = refs
+def place_last(early, late, before, target, sem):
     n, rows = early.shape[0], early.shape[1]
     chips = n // 2
-    early_rows = 2 * (rows // (2 * chunks_of(rows))) * extra_steps(rows)
+    share = rows // chunks_of(rows)
+    both, extra = value_split(rows)
     me = lax.axis_index("shard")
     chip, core = me // 2, lax.rem(me, 2)
 
-    def put(source, owner, *at):
-        where = (owner, *at)
-        pltpu.make_async_copy(source.at[where], target.at[where], sem.at[0]).start()
-
-    put(early, me)
-    put(early, me + 1 - 2 * core)
+    def put(source, owner, start, stop):
+        if start < stop:
+            where = owner, pl.ds(start * share, (stop - start) * share)
+            pltpu.make_async_copy(source.at[where], target.at[where], sem.at[0]).start()
+
+    count = rows // share
     for offset in range(1, chips):
         other = lax.rem(chip + offset, chips) * 2
-        put(late, other + 1 - core)
+        put(late, other + 1 - core, both, count)
 
         @pl.when(core == LEAD)
         def _():
-            put(late, other + core)
+            put(late, other + core, both, count)
 
         @pl.when(core != LEAD)
         def _():
-            if early_rows > 0:
-                put(early, other + core, pl.ds(0, early_rows))
-            put(late, other + core, pl.ds(early_rows, rows - early_rows))
-
-    pltpu.make_async_copy(late, late, sem.at[0]).wait()
+            put(early, other + core, both, both + extra)
+            put(late, other + core, both + extra, count)
+
+    part = late.at[pl.ds(0, n - 2), pl.ds(both * share, rows - both * share)]
+    pltpu.make_async_copy(part, part, sem.at[0]).wait()
 
 
 def body(n, width, w_query, low_query, high_query, w_key, low_key, high_key, w_value, low_value, high_value, norm_train, norm_step):
@@ -745,13 +774,13 @@
             pltpu.VMEM((3, rounds + 1, 1, columns), jnp.float32),
             pltpu.SemaphoreType.DMA((4, 3)),
             pltpu.SemaphoreType.DMA((4,)),
-            pltpu.SemaphoreType.DMA((2,)),
+            pltpu.SemaphoreType.DMA((3,)),
             pltpu.SemaphoreType.DMA((1,)),
             pltpu.SemaphoreType.DMA((3, rounds)),
             pltpu.SemaphoreType.DMA((1,)),
             pltpu.SemaphoreType.DMA((rounds,)),
             pltpu.SemaphoreType.DMA((5, slots)),
-            pltpu.SemaphoreType.DMA((2,)),
+            pltpu.SemaphoreType.DMA((3,)),
             pltpu.VMEM((3, rank, rows), jnp.bfloat16),
             pltpu.VMEM((3, 1, columns), jnp.float32),
             pltpu.VMEM((width, n, 1, length), jnp.float32),
@@ -774,16 +803,16 @@
         high_query, high_key, high_value,
         norm_train.reshape(1, length), norm_step.reshape(1, length),
     )
-    query, key, *small = pl.pallas_call(
+    query, key, value, *small = pl.pallas_call(
         place_first,
         name="place_first",
-        out_shape=[block] * 2
+        out_shape=[block] * 3
         + [jax.ShapeDtypeStruct((columns,), jnp.float32)] * 3
         + [jax.ShapeDtypeStruct((n * width * length,), jnp.bfloat16)],
-        in_specs=[ANY] + [HBM] * 2,
-        out_specs=[HBM] * 6,
+        in_specs=[ANY] * 2 + [HBM] * 2,
+        out_specs=[HBM] * 7,
         scratch_shapes=[
-            pltpu.SemaphoreType.DMA((3,)),
+            pltpu.SemaphoreType.DMA((5,)),
             pltpu.VMEM((3, 1, columns), jnp.float32),
             pltpu.VMEM((width, n, 1, length), jnp.float32),
             pltpu.SemaphoreType.DMA((6,)),
@@ -791,7 +820,7 @@
             pltpu.VMEM((n * width * length,), jnp.bfloat16),
         ],
         compiler_params=pltpu.CompilerParams(vmem_limit_bytes=2**20),
-    )(near(ready), far(factors), far(gains))
+    )(near(ready), near(early), far(factors), far(gains))
     late = pl.pallas_call(
         functools.partial(late_kernel, n),
         name="gather_late",
@@ -813,11 +842,12 @@
         place_last,
         name="place_last",
         out_shape=block,
-        in_specs=[ANY] * 2,
+        in_specs=[ANY] * 2 + [HBM],
         out_specs=HBM,
         scratch_shapes=[pltpu.SemaphoreType.DMA((1,))],
+        input_output_aliases={2: 0},
         compiler_params=pltpu.CompilerParams(vmem_limit_bytes=2**20),
-    )(near(early), near(late))
+    )(near(early), near(late), far(value))
     return (
         *(ready.reshape(n * rows, columns) for ready in (query, key, value)),
         *small,

time: 174 us -> 169 us (0.971)
  Pallas kernels: 174 us -> 169 us
    pallas_call x1, Pallas kernels: 31.9 us -> 16.1 us  [body(): pl.pallas_call(functools.partial(late_kernel, n), name='gather_late', out...]
    pallas_call x1, Pallas kernels: 128 us -> 139 us  [body(): pl.pallas_call(functools.partial(gather_kernel, n, width), name='merge_ga...]
where the time goes in v3:
time: 169 us
  Pallas kernels  169 us (100%)
    pallas_call x1, Pallas kernels, body(): pl.pallas_call(functools.partial(gather_kernel, n, width), name='merge_ga...  139 us
    pallas_call x1, Pallas kernels, body(): pl.pallas_call(functools.partial(late_kernel, n), name='gather_late', out...  16.1 us
    pallas_call x1, Pallas kernels, body(): pl.pallas_call(place_first, name='place_first', out_shape=[block] * 3 + [...  10.3 us

profile of v3, /device:TPU:0, one launch (start us, length us, event | category | flops | bytes accessed | tf_op | source)
XLA Modules:
  0.0 169.3 jit_solution(1738598955656817611)
XLA Ops:
  0.6 139.0 %merge_gather.1 = (bf16[2,8,640,1280]{3,2,1,0:T(8,128)(2,1)S(1)}, bf16[8,640,1280]{2,1,0:T(8,128)(2,1)S(1)}, f32[3,1,1280]{2,1,0:T(1,128)}, f32[4,8,1,160]{3,2,1,0:T(1,128)}) custom-call(bf16[640,1280]{1,0:T(8,128)(2,1)} %refs_0_.1, bf16[640,1280]{1,0:T(8,128)(2,1)} %refs_1_.1, bf16[640,1280]{1,0:T(8,128)(2,1)} %refs_2_.1, bf16[32,640]{1,0:T(8,128)(2,1)} %bitcast.9, ...), custom_call_target="tpu_custom_call" | custom-call | tf_op jit(solution)/shard_map/merge_gather/pallas_call | solution.py:756
  139.7 10.3 %place_first.1 = (bf16[8,640,1280]{2,1,0:T(8,128)(2,1)}, bf16[8,640,1280]{2,1,0:T(8,128)(2,1)}, bf16[8,640,1280]{2,1,0:T(8,128)(2,1)}, f32[1280]{0:T(1024)}, f32...) custom-call(bf16[2,8,640,1280]{3,2,1,0:T(8,128)(2,1)S(1)} %get-tuple-element.18.refs_0_, ...), custom_call_target="tpu_custom_call" | custom-call | tf_op jit(solution)/shard_map/place_first/pallas_call | solution.py:806
  150.0 16.1 %gather_late.1.late = bf16[8,640,1280]{2,1,0:T(8,128)(2,1)S(1)} custom-call(bf16[8,640,1280]{2,1,0:T(8,128)(2,1)S(1)} %get-tuple-element.19.refs_1_.refs_0_.early, f32[1280]{0:T(1024)} %get-tuple-element.14.refs_1_), custom_call_target="tpu_custom_call" | custom-call | tf_op jit(solution)/shard_map/gather_late/pallas_call | solution.py:824
  166.1 3.2 %place_last.1 = bf16[8,640,1280]{2,1,0:T(8,128)(2,1)} custom-call(bf16[8,640,1280]{2,1,0:T(8,128)(2,1)S(1)} %get-tuple-element.19.refs_1_.refs_0_.early, bf16[8,640,1280]{2,1,0:T(8,128)(2,1)S(1)} %gather_late.1.late, bf16[8,640,1280]{2,1,0:T(8,128)(2,1)} %get-tuple-element.25.before), custom_call_target="tpu_custom_call", output_to_operand_aliasing={{}: (2, {})} | custom-call | tf_op jit(solution)/shard_map/place_last/pallas_call | solution.py:841

commit v4 on v3

--- a/solution.py
+++ b/solution.py
@@ -9,7 +9,11 @@
 
 mix_rate = 0.5
 LEAD = 1
-BOTH = 1
+FINER = 1
+LAST = 16
+JOIN = 4
+BOTH = 2
+EXTRA = 6
 MESH = pl.DeviceIdType.MESH
 ANY = pl.BlockSpec(memory_space=pl.ANY)
 HBM = pl.BlockSpec(memory_space=pltpu.HBM)
@@ -22,14 +26,12 @@
     return 1
 
 
-def raw_steps(rows):
-    return min(2, chunks_of(rows))
-
-
 def value_split(rows):
-    count = chunks_of(rows)
-    extra = 3 * count // 5
-    return min(count // 5 * BOTH, count - extra), extra
+    count = FINER * chunks_of(rows)
+    if rows % (2 * count * 16) != 0:
+        count = chunks_of(rows)
+    extra = EXTRA * count // 10
+    return count, min(count * BOTH // 10, count - extra), extra
 
 
 def ring_slots(half):
@@ -55,10 +57,10 @@
     half = chips // 2
     count = chunks_of(rows)
     piece = rows // (2 * count)
-    both, extra = value_split(rows)
+    value_count, both, extra = value_split(rows)
+    value_piece = rows // (2 * value_count)
     shared = 2 * count + both
-    both_rows = 2 * piece * both
-    raw = raw_steps(rows)
+    raw = 1
     raw_rows = 2 * piece * raw
     reach = low_raw.shape[2]
     rounds = n.bit_length() - 1
@@ -247,15 +249,20 @@
     errands += [functools.partial(gain_line, s) for s in range(width - 1)]
 
     def rows_of(letter, k):
-        return (2 * (k % count) + letter) * piece
+        if k < 2 * count:
+            return pl.ds((2 * (k % count) + letter) * piece, piece)
+        return pl.ds((2 * (k - 2 * count) + letter) * value_piece, value_piece)
+
+    def matrix_of(k):
+        return min(k // count, 2)
 
     def finish(k):
         m = k // count
-        at = pl.ds(rows_of(0, k), 2 * piece)
+        at = pl.ds(2 * (k % count) * piece, 2 * piece)
         outs[m][me, at, :] = (latest[m, at, :] * scale[m]).astype(jnp.bfloat16)
 
     def view(k, letter, owner):
-        return outs[k // count].at[owner, pl.ds(rows_of(letter, k), piece)]
+        return outs[matrix_of(k)].at[owner, rows_of(letter, k)]
 
     def landing(k, side, letter, hop):
         return ring_sem.at[k % ring_sem.shape[0], slots.index((side, letter, hop))]
@@ -266,8 +273,8 @@
         where = view(k, letter, owner)
         source = where
         if k < raw and hop == 0:
-            source = w_mem.at[0, pl.ds(rows_of(letter, k), piece)]
-        sent = ring_send.at[k // count]
+            source = w_mem.at[0, rows_of(letter, k)]
+        sent = ring_send.at[matrix_of(k)]
         if k < raw:
             sent = ring_send.at[3]
             if hop > 0:
@@ -317,8 +324,8 @@
         pltpu.make_async_remote_copy(
             src_ref=where,
             dst_ref=where,
-            send_sem=pair_send.at[k // (2 * count) * 2],
-            recv_sem=pair_sem.at[k // (2 * count) * 2],
+            send_sem=pair_send.at[matrix_of(k) // 2 * 2],
+            recv_sem=pair_sem.at[matrix_of(k) // 2 * 2],
             device_id={"shard": sibling},
             device_id_type=MESH,
         ).start()
@@ -362,7 +369,7 @@
                 if (from_side, h) not in low_seen:
                     low_seen.add((from_side, h))
                     low_arrival(from_side, h)
-            at = pl.ds(rows_of(letter, k), piece)
+            at = rows_of(letter, k)
             value = ready[0, owner, at, :].astype(jnp.float32) + mix_rate * jnp.dot(
                 low_far[owner, at, :], high_mem[0], preferred_element_type=jnp.float32
             )
@@ -384,6 +391,12 @@
     closed = set()
     last_hops = [s for side in range(2) for s in slots[::-1] if s[0] == side and s[2] == hops(*s[0:2]) - 1]
 
+    def pass_on(k, hop):
+        for side in range(2):
+            owner = ring_arrival(k, side, side, hop)
+            ring_start(k, side, side, hop + 1)
+            landed(k, side, side, hop, owner)
+
     def close(k, side, letter, hop):
         closed.add((k, side, letter))
         landed(k, side, letter, hop, ring_arrival(k, side, letter, hop))
@@ -396,19 +409,15 @@
 
         if j < shared + extra and j != shared:
             by_role(j)(first_own)
-        if j == 1:
-            merge(1)
+        if j == 0:
+            merge(0)
             advance(0)
         for hop in range(half - 1):
             k = j - 1 - hop
+            if (k, hop) == (0, 0):
+                continue
             if 0 <= k < shared + extra:
-
-                @by_role(k)
-                def _():
-                    for side in range(2):
-                        owner = ring_arrival(k, side, side, hop)
-                        ring_start(k, side, side, hop + 1)
-                        landed(k, side, side, hop, owner)
+                by_role(k)(functools.partial(pass_on, k, hop))
 
         if j == shared and extra > 0:
             by_role(j)(first_own)
@@ -435,13 +444,14 @@
             for letter in range(2):
                 pair_copy(j, letter, me)
         if j == 0:
-            merge(0)
             for side in range(2):
                 if hops(side, 0) > 0:
                     low_copy(side, 0).start()
             advance(0)
-        if j == raw:
-            merge(2)
+            if half > 1:
+                pass_on(0, 0)
+        if j in (1, 2):
+            merge(j)
         for m in range(1, 3):
             if j > m and met[m] < rounds:
                 advance(m)
@@ -489,7 +499,7 @@
     own_value[0].wait_send()
 
     def value_part(share):
-        return early.at[pl.ds(0, chips - 1), pl.ds(0, share * 2 * piece)]
+        return early.at[pl.ds(0, chips - 1), pl.ds(0, share * 2 * value_piece)]
 
     if both > 0:
         theirs = value_part(both)
@@ -521,13 +531,13 @@
 
 def late_kernel(n, *refs):
     early, late = refs[0], refs[2]
-    ring_send, pair_send, pair_sem, ring_sem, joined = refs[3:8]
+    ring_send, pair_send, pair_sem, ring_sem, joined, last_sem = refs[3:9]
+    parts = last_sem.shape[1]
     rows = early.shape[1]
     chips = n // 2
     half = chips // 2
-    count = chunks_of(rows)
+    count, both, extra = value_split(rows)
     piece = rows // (2 * count)
-    both, extra = value_split(rows)
     slots = ring_slots(half)
 
     me = lax.axis_index("shard")
@@ -545,28 +555,41 @@
     def hops(side, letter):
         return half if side == letter else half - 1
 
-    def view(ref, k, letter, owner):
-        return ref.at[owner, pl.ds((2 * k + letter) * piece, piece)]
-
-    def ring_copy(k, side, letter, hop):
+    def view(ref, k, letter, owner, part=None):
+        first, size = (2 * k + letter) * piece, piece
+        if part is not None:
+            size = piece // parts
+            first += part * size
+        return ref.at[owner, pl.ds(first, size)]
+
+    def landing(k, side, letter, hop, part=None):
+        if part is not None:
+            return last_sem.at[side, part]
+        return ring_sem.at[k % ring_sem.shape[0], slots.index((side, letter, hop))]
+
+    def cut(k, side, letter, hop):
+        if k == count - 1 and side == letter and hop == half - 1 and hop > 0 and parts > 1:
+            return range(parts)
+        return [None]
+
+    def ring_start(k, side, letter, hop):
         sign = 1 - 2 * side
         owner = shard_at(-sign * hop)
-        return pltpu.make_async_remote_copy(
-            src_ref=view(early if hop == 0 else late, k, letter, owner),
-            dst_ref=view(late, k, letter, owner),
-            send_sem=ring_send.at[0],
-            recv_sem=ring_sem.at[k, slots.index((side, letter, hop))],
-            device_id={"shard": shard_at(sign)},
-            device_id_type=MESH,
-        )
-
-    def ring_arrival(k, side, letter, hop):
+        for part in cut(k, side, letter, hop):
+            pltpu.make_async_remote_copy(
+                src_ref=view(early if hop == 0 else late, k, letter, owner, part),
+                dst_ref=view(late, k, letter, owner, part),
+                send_sem=ring_send.at[0],
+                recv_sem=landing(k, side, letter, hop, part),
+                device_id={"shard": shard_at(sign)},
+                device_id_type=MESH,
+            ).start()
+
+    def ring_arrival(k, side, letter, hop, part=None):
         sign = 1 - 2 * side
-        owner = shard_at(-sign * (hop + 1))
-        where = view(late, k, letter, owner)
-        landed = ring_sem.at[k, slots.index((side, letter, hop))]
-        pltpu.make_async_copy(where, where, landed).wait()
-        return owner
+        where = view(late, k, letter, shard_at(-sign * (hop + 1)), part)
+        pltpu.make_async_copy(where, where, landing(k, side, letter, hop, part)).wait()
+        return where
 
     def to_sibling(source, target):
         pltpu.make_async_remote_copy(
@@ -587,8 +610,7 @@
     def run(first, join):
         waiting = []
 
-        def landed(k, letter, owner):
-            where = view(late, k, letter, owner)
+        def landed(where):
             if join is not None and not joined_at:
                 waiting.append(where)
             else:
@@ -599,36 +621,41 @@
             if j < count:
                 for side in range(2):
                     if hops(side, side) > 0:
-                        ring_copy(j, side, side, 0).start()
+                        ring_start(j, side, side, 0)
             for hop in range(half - 1):
                 k = j - 1 - hop
                 if first <= k < count:
                     for side in range(2):
-                        owner = ring_arrival(k, side, side, hop)
-                        ring_copy(k, side, side, hop + 1).start()
-                        landed(k, side, owner)
+                        where = ring_arrival(k, side, side, hop)
+                        ring_start(k, side, side, hop + 1)
+                        landed(where)
             if j < count:
                 for side in range(2):
                     if hops(side, 1 - side) > 0:
-                        ring_copy(j, side, 1 - side, 0).start()
+                        ring_start(j, side, 1 - side, 0)
             for hop in range(half - 2):
                 k = j - 1 - hop
                 if first <= k < count:
                     for side in range(2):
-                        owner = ring_arrival(k, side, 1 - side, hop)
-                        ring_copy(k, side, 1 - side, hop + 1).start()
-                        landed(k, 1 - side, owner)
+                        where = ring_arrival(k, side, 1 - side, hop)
+                        ring_start(k, side, 1 - side, hop + 1)
+                        landed(where)
             if j == join:
                 pl.semaphore_wait(joined, 1)
                 joined_at.append(j)
                 for where in waiting:
                     to_sibling(where, where)
-            for side in range(2):
-                for letter in (side, 1 - side):
-                    hop = hops(side, letter) - 1
-                    k = j - 1 - hop
-                    if hop >= 0 and first <= k < count:
-                        landed(k, letter, ring_arrival(k, side, letter, hop))
+            ends = [
+                (j - hops(side, letter), side, letter, hops(side, letter) - 1)
+                for flip in range(2)
+                for side in range(2)
+                for letter in (side ^ flip,)
+            ]
+            ends = [s for s in ends if s[3] >= 0 and first <= s[0] < count]
+            for part in range(parts):
+                for s in ends:
+                    if part < len(cut(*s)):
+                        landed(ring_arrival(*s, cut(*s)[part]))
         if first < count:
             sent = late.at[pl.ds(0, chips - 1), pl.ds(0, 2 * piece * (count - first))]
             pltpu.make_async_copy(sent, sent, ring_send.at[0]).wait()
@@ -637,7 +664,7 @@
     def _():
         pl.semaphore_signal(barrier, inc=1, device_id={"shard": sibling}, device_id_type=MESH)
         pl.semaphore_wait(barrier, 2)
-        run(both, count - 1 if both + extra < count else count)
+        run(both, JOIN)
 
     @pl.when(core != LEAD)
     def _():
@@ -667,7 +694,8 @@
         pltpu.make_async_copy(small[i], refs[12 + i], small_sem.at[i]) for i in range(2)
     ]
     n, rows = early.shape[0], early.shape[1]
-    both_rows = rows // chunks_of(rows) * value_split(rows)[0]
+    value_count, both, _ = value_split(rows)
+    both_rows = rows // value_count * both
     chip = lax.div(lax.axis_index("shard"), 2)
     copies = [
         pltpu.make_async_copy(source.at[m, i], targets[m].at[i], sem.at[2 if m else min(i, 1)])
@@ -693,9 +721,9 @@
     for copy in writes:
         copy.start()
     rest = source.at[0, pl.ds(1, source.shape[1] - 1)]
-    both = source.at[1]
+    second = source.at[1]
     pltpu.make_async_copy(rest, rest, sem.at[1]).wait()
-    pltpu.make_async_copy(both, both, sem.at[2]).wait()
+    pltpu.make_async_copy(second, second, sem.at[2]).wait()
     pltpu.make_async_copy(early.at[ours], targets[2].at[ours], sem.at[3]).wait()
     if both_rows > 0:
         part = early.at[pl.ds(0, n - 2), pl.ds(0, both_rows)]
@@ -707,8 +735,8 @@
 def place_last(early, late, before, target, sem):
     n, rows = early.shape[0], early.shape[1]
     chips = n // 2
-    share = rows // chunks_of(rows)
-    both, extra = value_split(rows)
+    count, both, extra = value_split(rows)
+    share = rows // count
     me = lax.axis_index("shard")
     chip, core = me // 2, lax.rem(me, 2)
 
@@ -717,7 +745,6 @@
             where = owner, pl.ds(start * share, (stop - start) * share)
             pltpu.make_async_copy(source.at[where], target.at[where], sem.at[0]).start()
 
-    count = rows // share
     for offset in range(1, chips):
         other = lax.rem(chip + offset, chips) * 2
         put(late, other + 1 - core, both, count)
@@ -741,7 +768,7 @@
     length = norm_train.shape[0]
     half = n // 4
     count = chunks_of(rows)
-    raw = raw_steps(rows)
+    raw = 1
     rounds = n.bit_length() - 1
     reach = min(rows, -(-(rows // count) * raw // 128) * 128)
     slots = len(ring_slots(half))
@@ -831,8 +858,9 @@
             pltpu.SemaphoreType.DMA((1,)),
             pltpu.SemaphoreType.DMA((1,)),
             pltpu.SemaphoreType.DMA((1,)),
-            pltpu.SemaphoreType.DMA((count, slots)),
+            pltpu.SemaphoreType.DMA((5, slots)),
             pltpu.SemaphoreType.REGULAR,
+            pltpu.SemaphoreType.DMA((2, max(rows // (2 * value_split(rows)[0] * LAST), 1))),
         ],
         compiler_params=pltpu.CompilerParams(
             collective_id=1, has_side_effects=True, vmem_limit_bytes=2**20

time: 169 us -> 169 us (level)
  no operation moved by 1% of the time
where the time goes in v4:
time: 169 us
  Pallas kernels  168 us (99%)
    pallas_call x1, Pallas kernels, body(): pl.pallas_call(functools.partial(gather_kernel, n, width), name='merge_ga...  139 us
    pallas_call x1, Pallas kernels, body(): pl.pallas_call(functools.partial(late_kernel, n), name='gather_late', out...  15.8 us
    pallas_call x1, Pallas kernels, body(): pl.pallas_call(place_first, name='place_first', out_shape=[block] * 3 + [...  10.3 us

profile of v4, /device:TPU:0, one launch (start us, length us, event | category | flops | bytes accessed | tf_op | source)
XLA Modules:
  0.0 168.6 jit_solution(15353454226976273009)
XLA Ops:
  0.6 138.7 %merge_gather.1 = (bf16[2,8,640,1280]{3,2,1,0:T(8,128)(2,1)S(1)}, bf16[8,640,1280]{2,1,0:T(8,128)(2,1)S(1)}, f32[3,1,1280]{2,1,0:T(1,128)}, f32[4,8,1,160]{3,2,1,0:T(1,128)}) custom-call(bf16[640,1280]{1,0:T(8,128)(2,1)} %refs_0_.1, bf16[640,1280]{1,0:T(8,128)(2,1)} %refs_1_.1, bf16[640,1280]{1,0:T(8,128)(2,1)} %refs_2_.1, bf16[32,640]{1,0:T(8,128)(2,1)} %bitcast.9, ...), custom_call_target="tpu_custom_call" | custom-call | tf_op jit(solution)/shard_map/merge_gather/pallas_call | solution.py:783
  139.3 10.3 %place_first.1 = (bf16[8,640,1280]{2,1,0:T(8,128)(2,1)}, bf16[8,640,1280]{2,1,0:T(8,128)(2,1)}, bf16[8,640,1280]{2,1,0:T(8,128)(2,1)}, f32[1280]{0:T(1024)}, f32...) custom-call(bf16[2,8,640,1280]{3,2,1,0:T(8,128)(2,1)S(1)} %get-tuple-element.18.refs_0_, ...), custom_call_target="tpu_custom_call" | custom-call | tf_op jit(solution)/shard_map/place_first/pallas_call | solution.py:833
  149.7 15.8 %gather_late.1.late = bf16[8,640,1280]{2,1,0:T(8,128)(2,1)S(1)} custom-call(bf16[8,640,1280]{2,1,0:T(8,128)(2,1)S(1)} %get-tuple-element.19.refs_1_.refs_0_.early, f32[1280]{0:T(1024)} %get-tuple-element.14.refs_1_), custom_call_target="tpu_custom_call" | custom-call | tf_op jit(solution)/shard_map/gather_late/pallas_call | solution.py:851
  165.5 3.2 %place_last.1 = bf16[8,640,1280]{2,1,0:T(8,128)(2,1)} custom-call(bf16[8,640,1280]{2,1,0:T(8,128)(2,1)S(1)} %get-tuple-element.19.refs_1_.refs_0_.early, bf16[8,640,1280]{2,1,0:T(8,128)(2,1)S(1)} %gather_late.1.late, bf16[8,640,1280]{2,1,0:T(8,128)(2,1)} %get-tuple-element.25.before), custom_call_target="tpu_custom_call", output_to_operand_aliasing={{}: (2, {})} | custom-call | tf_op jit(solution)/shard_map/place_last/pallas_call | solution.py:869

commit v5 on v4

--- a/solution.py
+++ b/solution.py
@@ -9,11 +9,10 @@
 
 mix_rate = 0.5
 LEAD = 1
-FINER = 1
-LAST = 16
-JOIN = 4
+SIZES = (2, 1, 2, 2, 2, 1)
+JOIN = 6
 BOTH = 2
-EXTRA = 6
+EXTRA = 3
 MESH = pl.DeviceIdType.MESH
 ANY = pl.BlockSpec(memory_space=pl.ANY)
 HBM = pl.BlockSpec(memory_space=pltpu.HBM)
@@ -27,11 +26,18 @@
 
 
 def value_split(rows):
-    count = FINER * chunks_of(rows)
-    if rows % (2 * count * 16) != 0:
-        count = chunks_of(rows)
-    extra = EXTRA * count // 10
-    return count, min(count * BOTH // 10, count - extra), extra
+    sizes = SIZES
+    if rows % (sum(sizes) * 32) != 0:
+        sizes = [1] * chunks_of(rows)
+    unit = rows // sum(sizes)
+    starts = [unit * sum(sizes[:i]) for i in range(len(sizes) + 1)]
+    extra = min(EXTRA, len(sizes) - 1)
+    return starts, min(BOTH, len(sizes) - extra), extra
+
+
+def last_parts(rows):
+    starts = value_split(rows)[0]
+    return max((rows - starts[-2]) // 32, 1)
 
 
 def ring_slots(half):
@@ -57,8 +63,7 @@
     half = chips // 2
     count = chunks_of(rows)
     piece = rows // (2 * count)
-    value_count, both, extra = value_split(rows)
-    value_piece = rows // (2 * value_count)
+    starts, both, extra = value_split(rows)
     shared = 2 * count + both
     raw = 1
     raw_rows = 2 * piece * raw
@@ -251,7 +256,8 @@
     def rows_of(letter, k):
         if k < 2 * count:
             return pl.ds((2 * (k % count) + letter) * piece, piece)
-        return pl.ds((2 * (k - 2 * count) + letter) * value_piece, value_piece)
+        first, stop = starts[k - 2 * count : k - 2 * count + 2]
+        return pl.ds(first + letter * (stop - first) // 2, (stop - first) // 2)
 
     def matrix_of(k):
         return min(k // count, 2)
@@ -499,7 +505,7 @@
     own_value[0].wait_send()
 
     def value_part(share):
-        return early.at[pl.ds(0, chips - 1), pl.ds(0, share * 2 * value_piece)]
+        return early.at[pl.ds(0, chips - 1), pl.ds(0, starts[share])]
 
     if both > 0:
         theirs = value_part(both)
@@ -536,8 +542,8 @@
     rows = early.shape[1]
     chips = n // 2
     half = chips // 2
-    count, both, extra = value_split(rows)
-    piece = rows // (2 * count)
+    starts, both, extra = value_split(rows)
+    count = len(starts) - 1
     slots = ring_slots(half)
 
     me = lax.axis_index("shard")
@@ -556,9 +562,10 @@
         return half if side == letter else half - 1
 
     def view(ref, k, letter, owner, part=None):
-        first, size = (2 * k + letter) * piece, piece
+        size = (starts[k + 1] - starts[k]) // 2
+        first = starts[k] + letter * size
         if part is not None:
-            size = piece // parts
+            size = size // parts
             first += part * size
         return ref.at[owner, pl.ds(first, size)]
 
@@ -657,7 +664,7 @@
                     if part < len(cut(*s)):
                         landed(ring_arrival(*s, cut(*s)[part]))
         if first < count:
-            sent = late.at[pl.ds(0, chips - 1), pl.ds(0, 2 * piece * (count - first))]
+            sent = late.at[pl.ds(0, chips - 1), pl.ds(0, rows - starts[first])]
             pltpu.make_async_copy(sent, sent, ring_send.at[0]).wait()
 
     @pl.when(core == LEAD)
@@ -673,11 +680,11 @@
         if extra > 0:
             for offset in range(1, chips):
                 owner = shard_at(offset)
-                at = pl.ds(2 * piece * both, 2 * piece * extra)
+                at = pl.ds(starts[both], starts[both + extra] - starts[both])
                 to_sibling(early.at[owner, at], late.at[owner, at])
         run(both + extra, None)
 
-    theirs = late.at[pl.ds(0, chips - 1), pl.ds(0, 2 * piece * (count - both))]
+    theirs = late.at[pl.ds(0, chips - 1), pl.ds(0, rows - starts[both])]
     pltpu.make_async_copy(theirs, theirs, pair_sem.at[0]).wait()
     pltpu.make_async_copy(theirs, theirs, pair_send.at[0]).wait()
 
@@ -694,8 +701,8 @@
         pltpu.make_async_copy(small[i], refs[12 + i], small_sem.at[i]) for i in range(2)
     ]
     n, rows = early.shape[0], early.shape[1]
-    value_count, both, _ = value_split(rows)
-    both_rows = rows // value_count * both
+    starts, both, _ = value_split(rows)
+    both_rows = starts[both]
     chip = lax.div(lax.axis_index("shard"), 2)
     copies = [
         pltpu.make_async_copy(source.at[m, i], targets[m].at[i], sem.at[2 if m else min(i, 1)])
@@ -735,16 +742,16 @@
 def place_last(early, late, before, target, sem):
     n, rows = early.shape[0], early.shape[1]
     chips = n // 2
-    count, both, extra = value_split(rows)
-    share = rows // count
+    starts, both, extra = value_split(rows)
     me = lax.axis_index("shard")
     chip, core = me // 2, lax.rem(me, 2)
 
     def put(source, owner, start, stop):
         if start < stop:
-            where = owner, pl.ds(start * share, (stop - start) * share)
+            where = owner, pl.ds(starts[start], starts[stop] - starts[start])
             pltpu.make_async_copy(source.at[where], target.at[where], sem.at[0]).start()
 
+    count = len(starts) - 1
     for offset in range(1, chips):
         other = lax.rem(chip + offset, chips) * 2
         put(late, other + 1 - core, both, count)
@@ -758,7 +765,7 @@
             put(early, other + core, both, both + extra)
             put(late, other + core, both + extra, count)
 
-    part = late.at[pl.ds(0, n - 2), pl.ds(both * share, rows - both * share)]
+    part = late.at[pl.ds(0, n - 2), pl.ds(starts[both], rows - starts[both])]
     pltpu.make_async_copy(part, part, sem.at[0]).wait()
 
 
@@ -772,6 +779,7 @@
     rounds = n.bit_length() - 1
     reach = min(rows, -(-(rows // count) * raw // 128) * 128)
     slots = len(ring_slots(half))
+    starts, both, _ = value_split(rows)
     block = jax.ShapeDtypeStruct((n, rows, columns), jnp.bfloat16)
 
     def near(value):
@@ -858,9 +866,9 @@
             pltpu.SemaphoreType.DMA((1,)),
             pltpu.SemaphoreType.DMA((1,)),
             pltpu.SemaphoreType.DMA((1,)),
-            pltpu.SemaphoreType.DMA((5, slots)),
+            pltpu.SemaphoreType.DMA((len(starts) - 1 - both, slots)),
             pltpu.SemaphoreType.REGULAR,
-            pltpu.SemaphoreType.DMA((2, max(rows // (2 * value_split(rows)[0] * LAST), 1))),
+            pltpu.SemaphoreType.DMA((2, last_parts(rows))),
         ],
         compiler_params=pltpu.CompilerParams(
             collective_id=1, has_side_effects=True, vmem_limit_bytes=2**20

time: 169 us -> 169 us (level)
    pallas_call x1, Pallas kernels: 15.8 us -> 10.5 us  [body(): pl.pallas_call(functools.partial(late_kernel, n), name='gather_late', out...]
    pallas_call x1, Pallas kernels: 139 us -> 144 us  [body(): pl.pallas_call(functools.partial(gather_kernel, n, width), name='merge_ga...]
where the time goes in v5:
time: 169 us
  Pallas kernels  168 us (99%)
    pallas_call x1, Pallas kernels, body(): pl.pallas_call(functools.partial(gather_kernel, n, width), name='merge_ga...  144 us
    pallas_call x1, Pallas kernels, body(): pl.pallas_call(place_first, name='place_first', out_shape=[block] * 3 + [...  10.7 us
    pallas_call x1, Pallas kernels, body(): pl.pallas_call(functools.partial(late_kernel, n), name='gather_late', out...  10.5 us

profile of v5, /device:TPU:0, one launch (start us, length us, event | category | flops | bytes accessed | tf_op | source)
XLA Modules:
  0.0 168.5 jit_solution(2657266353362526235)
XLA Ops:
  0.6 143.9 %merge_gather.1 = (bf16[2,8,640,1280]{3,2,1,0:T(8,128)(2,1)S(1)}, bf16[8,640,1280]{2,1,0:T(8,128)(2,1)S(1)}, f32[3,1,1280]{2,1,0:T(1,128)}, f32[4,8,1,160]{3,2,1,0:T(1,128)}) custom-call(bf16[640,1280]{1,0:T(8,128)(2,1)} %refs_0_.1, bf16[640,1280]{1,0:T(8,128)(2,1)} %refs_1_.1, bf16[640,1280]{1,0:T(8,128)(2,1)} %refs_2_.1, bf16[32,640]{1,0:T(8,128)(2,1)} %bitcast.9, ...), custom_call_target="tpu_custom_call" | custom-call | tf_op jit(solution)/shard_map/merge_gather/pallas_call | solution.py:791
  144.5 10.7 %place_first.1 = (bf16[8,640,1280]{2,1,0:T(8,128)(2,1)}, bf16[8,640,1280]{2,1,0:T(8,128)(2,1)}, bf16[8,640,1280]{2,1,0:T(8,128)(2,1)}, f32[1280]{0:T(1024)}, f32...) custom-call(bf16[2,8,640,1280]{3,2,1,0:T(8,128)(2,1)S(1)} %get-tuple-element.18.refs_0_, ...), custom_call_target="tpu_custom_call" | custom-call | tf_op jit(solution)/shard_map/place_first/pallas_call | solution.py:841
  155.2 10.5 %gather_late.1.late = bf16[8,640,1280]{2,1,0:T(8,128)(2,1)S(1)} custom-call(bf16[8,640,1280]{2,1,0:T(8,128)(2,1)S(1)} %get-tuple-element.19.refs_1_.refs_0_.early, f32[1280]{0:T(1024)} %get-tuple-element.14.refs_1_), custom_call_target="tpu_custom_call" | custom-call | tf_op jit(solution)/shard_map/gather_late/pallas_call | solution.py:859
  165.7 2.8 %place_last.1 = bf16[8,640,1280]{2,1,0:T(8,128)(2,1)} custom-call(bf16[8,640,1280]{2,1,0:T(8,128)(2,1)S(1)} %get-tuple-element.19.refs_1_.refs_0_.early, bf16[8,640,1280]{2,1,0:T(8,128)(2,1)S(1)} %gather_late.1.late, bf16[8,640,1280]{2,1,0:T(8,128)(2,1)} %get-tuple-element.25.before), custom_call_target="tpu_custom_call", output_to_operand_aliasing={{}: (2, {})} | custom-call | tf_op jit(solution)/shard_map/place_last/pallas_call | solution.py:877

commit v6 on v5

--- a/solution.py
+++ b/solution.py
@@ -105,8 +105,6 @@
             parts.append(load(weights[0].at[rest], w_mem.at[0, rest], m, 2))
         loads.append(parts)
     norm_loads = [load(norms[i], norm_mem.at[i], 3, i) for i in range(2)]
-    first.start()
-
     barrier = pltpu.get_barrier_semaphore()
 
     def greet(axis, index):
@@ -125,6 +123,7 @@
     def _():
         greet("width", line + 1)
 
+    first.start()
     for parts in loads:
         for copy in parts:
             copy.start()
@@ -748,8 +747,10 @@
 
     def put(source, owner, start, stop):
         if start < stop:
-            where = owner, pl.ds(starts[start], starts[stop] - starts[start])
-            pltpu.make_async_copy(source.at[where], target.at[where], sem.at[0]).start()
+            size = (starts[stop] - starts[start]) // 2
+            for part in range(2):
+                where = owner, pl.ds(starts[start] + part * size, size)
+                pltpu.make_async_copy(source.at[where], target.at[where], sem.at[0]).start()
 
     count = len(starts) - 1
     for offset in range(1, chips):

time: 169 us -> 169 us (level)
  no operation moved by 1% of the time
where the time goes in v6:
time: 169 us
  Pallas kernels  168 us (99%)
    pallas_call x1, Pallas kernels, body(): pl.pallas_call(functools.partial(gather_kernel, n, width), name='merge_ga...  144 us
    pallas_call x1, Pallas kernels, body(): pl.pallas_call(place_first, name='place_first', out_shape=[block] * 3 + [...  10.7 us
    pallas_call x1, Pallas kernels, body(): pl.pallas_call(functools.partial(late_kernel, n), name='gather_late', out...  10.5 us

profile of v6, /device:TPU:0, one launch (start us, length us, event | category | flops | bytes accessed | tf_op | source)
XLA Modules:
  0.0 168.5 jit_solution(4238536208587461499)
XLA Ops:
  0.6 143.9 %merge_gather.1 = (bf16[2,8,640,1280]{3,2,1,0:T(8,128)(2,1)S(1)}, bf16[8,640,1280]{2,1,0:T(8,128)(2,1)S(1)}, f32[3,1,1280]{2,1,0:T(1,128)}, f32[4,8,1,160]{3,2,1,0:T(1,128)}) custom-call(bf16[640,1280]{1,0:T(8,128)(2,1)} %refs_0_.1, bf16[640,1280]{1,0:T(8,128)(2,1)} %refs_1_.1, bf16[640,1280]{1,0:T(8,128)(2,1)} %refs_2_.1, bf16[32,640]{1,0:T(8,128)(2,1)} %bitcast.9, ...), custom_call_target="tpu_custom_call" | custom-call | tf_op jit(solution)/shard_map/merge_gather/pallas_call | solution.py:792
  144.5 10.7 %place_first.1 = (bf16[8,640,1280]{2,1,0:T(8,128)(2,1)}, bf16[8,640,1280]{2,1,0:T(8,128)(2,1)}, bf16[8,640,1280]{2,1,0:T(8,128)(2,1)}, f32[1280]{0:T(1024)}, f32...) custom-call(bf16[2,8,640,1280]{3,2,1,0:T(8,128)(2,1)S(1)} %get-tuple-element.18.refs_0_, ...), custom_call_target="tpu_custom_call" | custom-call | tf_op jit(solution)/shard_map/place_first/pallas_call | solution.py:842
  155.2 10.5 %gather_late.1.late = bf16[8,640,1280]{2,1,0:T(8,128)(2,1)S(1)} custom-call(bf16[8,640,1280]{2,1,0:T(8,128)(2,1)S(1)} %get-tuple-element.19.refs_1_.refs_0_.early, f32[1280]{0:T(1024)} %get-tuple-element.14.refs_1_), custom_call_target="tpu_custom_call" | custom-call | tf_op jit(solution)/shard_map/gather_late/pallas_call | solution.py:860
  165.7 2.8 %place_last.1 = bf16[8,640,1280]{2,1,0:T(8,128)(2,1)} custom-call(bf16[8,640,1280]{2,1,0:T(8,128)(2,1)S(1)} %get-tuple-element.19.refs_1_.refs_0_.early, bf16[8,640,1280]{2,1,0:T(8,128)(2,1)S(1)} %gather_late.1.late, bf16[8,640,1280]{2,1,0:T(8,128)(2,1)} %get-tuple-element.25.before), custom_call_target="tpu_custom_call", output_to_operand_aliasing={{}: (2, {})} | custom-call | tf_op jit(solution)/shard_map/place_last/pallas_call | solution.py:878

commit v7 on v6

--- a/solution.py
+++ b/solution.py
@@ -110,8 +110,9 @@
     def greet(axis, index):
         pl.semaphore_signal(barrier, inc=1, device_id={axis: index}, device_id_type=MESH)
 
-    greet("shard", shard_at(1))
-    greet("shard", shard_at(-1))
+    ring_greets = 0 if chips == 4 else 2
+    for offset in (1, -1)[:ring_greets]:
+        greet("shard", shard_at(offset))
     for r in range(rounds):
         greet("shard", partner(r))
 
@@ -389,7 +390,7 @@
     first.wait()
     pl.semaphore_wait(
         barrier,
-        2 + rounds + (line > 0).astype(jnp.int32) + (line < width - 1).astype(jnp.int32),
+        ring_greets + rounds + (line > 0).astype(jnp.int32) + (line < width - 1).astype(jnp.int32),
     )
 
     own_value = []

time: 169 us -> 169 us (level)
  no operation moved by 1% of the time
where the time goes in v7:
time: 169 us
  Pallas kernels  168 us (99%)
    pallas_call x1, Pallas kernels, body(): pl.pallas_call(functools.partial(gather_kernel, n, width), name='merge_ga...  144 us
    pallas_call x1, Pallas kernels, body(): pl.pallas_call(place_first, name='place_first', out_shape=[block] * 3 + [...  10.7 us
    pallas_call x1, Pallas kernels, body(): pl.pallas_call(functools.partial(late_kernel, n), name='gather_late', out...  10.5 us

profile of v7, /device:TPU:0, one launch (start us, length us, event | category | flops | bytes accessed | tf_op | source)
XLA Modules:
  0.0 168.5 jit_solution(11075364258675505512)
XLA Ops:
  0.6 143.8 %merge_gather.1 = (bf16[2,8,640,1280]{3,2,1,0:T(8,128)(2,1)S(1)}, bf16[8,640,1280]{2,1,0:T(8,128)(2,1)S(1)}, f32[3,1,1280]{2,1,0:T(1,128)}, f32[4,8,1,160]{3,2,1,0:T(1,128)}) custom-call(bf16[640,1280]{1,0:T(8,128)(2,1)} %refs_0_.1, bf16[640,1280]{1,0:T(8,128)(2,1)} %refs_1_.1, bf16[640,1280]{1,0:T(8,128)(2,1)} %refs_2_.1, bf16[32,640]{1,0:T(8,128)(2,1)} %bitcast.9, ...), custom_call_target="tpu_custom_call" | custom-call | tf_op jit(solution)/shard_map/merge_gather/pallas_call | solution.py:793
  144.5 10.7 %place_first.1 = (bf16[8,640,1280]{2,1,0:T(8,128)(2,1)}, bf16[8,640,1280]{2,1,0:T(8,128)(2,1)}, bf16[8,640,1280]{2,1,0:T(8,128)(2,1)}, f32[1280]{0:T(1024)}, f32...) custom-call(bf16[2,8,640,1280]{3,2,1,0:T(8,128)(2,1)S(1)} %get-tuple-element.18.refs_0_, ...), custom_call_target="tpu_custom_call" | custom-call | tf_op jit(solution)/shard_map/place_first/pallas_call | solution.py:843
  155.1 10.5 %gather_late.1.late = bf16[8,640,1280]{2,1,0:T(8,128)(2,1)S(1)} custom-call(bf16[8,640,1280]{2,1,0:T(8,128)(2,1)S(1)} %get-tuple-element.19.refs_1_.refs_0_.early, f32[1280]{0:T(1024)} %get-tuple-element.14.refs_1_), custom_call_target="tpu_custom_call" | custom-call | tf_op jit(solution)/shard_map/gather_late/pallas_call | solution.py:861
  165.7 2.8 %place_last.1 = bf16[8,640,1280]{2,1,0:T(8,128)(2,1)} custom-call(bf16[8,640,1280]{2,1,0:T(8,128)(2,1)S(1)} %get-tuple-element.19.refs_1_.refs_0_.early, bf16[8,640,1280]{2,1,0:T(8,128)(2,1)S(1)} %gather_late.1.late, bf16[8,640,1280]{2,1,0:T(8,128)(2,1)} %get-tuple-element.25.before), custom_call_target="tpu_custom_call", output_to_operand_aliasing={{}: (2, {})} | custom-call | tf_op jit(solution)/shard_map/place_last/pallas_call | solution.py:879
